TPU v7x, 512 devices: a whole 4x8x8 slice. The times are simulated.
512 devices in a mesh: section: 4 (over z_hi, core), pts: 128 (over x, z_lo, y).
Axes of the slice: x: 4, y: 8, z: 8 (z_hi: 2, z_lo: 4; z = z_hi * 4 + z_lo), core: 2. Of those that a mesh axis runs over, the one named last changes fastest.
Arguments:
- spectra: float32 [4, 12288, 1152], P('section', 'pts'), may hold values from 0.05 to 2
- neighbours: int32 [4, 12288], P(None, 'pts'), may hold values from 0 to 159, as said below
- upwind: int32 [4, 32, 12288], P(None, None, 'pts'), may hold values 0 or 1
- edge_weight: float32 [4, 12288], P(None, 'pts'), may hold values from 0.05 to 0.24
- edge_angle: float32 [4, 12288], P(None, 'pts'), may hold values from -3.140625 to 3.140625
- depth_class: int32 [12288], P('pts'), may hold values from 0 to 7
- class_table: float32 [4, 8, 36], P('section'), may hold values from 0.05 to 0.22
- section_point: float32 [4, 12288], P('section', 'pts'), may hold values from 0.5 to 2
- section_angle: float32 [4, 12288], P('section', 'pts'), may hold values from -3.140625 to 3.140625
Outputs:
- final_spectra: float32 [4, 12288, 1152], P('section', 'pts')
Inputs may be any that keep to these rules, and one draw needn't show every extreme that they name: neighbours[n, g] is a position in point g's tile of 96 points extended by 32 points of the tile before and the tile after it, never g's own position, and its neighbour lies within 32 points of g.
All inputs are finite; a program needn't handle non-finite values. No bound on the sum of `upwind` on one device may be relied on, other than what follows from the above.
Results may differ from a plain program's by a relative error of at most 0.00011.
Values sent between devices are 32-bit elements; how exact they have to be, the bound alone decides.
A program may use at most 64 MiB of HBM per device.

v0:
```python
import math

import jax
import jax.numpy as jnp
from jax import lax
from jax.sharding import PartitionSpec as P

HALO = 32
ADV_STEPS = 2


def with_halo(block, sides, width):
    for axis, dim in sides:
        count = lax.axis_size(axis)
        forward = [(i, i + 1) for i in range(count - 1)]
        backward = [(target, source) for source, target in forward]
        low = lax.ppermute(
            lax.slice_in_dim(block, block.shape[dim] - width, None, axis=dim), axis, forward
        )
        high = lax.ppermute(lax.slice_in_dim(block, 0, width, axis=dim), axis, backward)
        block = jnp.concatenate([low, block, high], axis=dim)
    return block


def side_by_side(arrays, axis, dim, along):
    widths = [math.prod(a.shape[along:]) for a in arrays]
    both = jnp.concatenate(
        [a.reshape(*a.shape[:along], w) for a, w in zip(arrays, widths)], axis=along
    )
    filled = lax.all_gather(both, axis, axis=dim, tiled=True)
    blocks = jnp.split(filled, [sum(widths[:k]) for k in range(1, len(widths))], axis=along)
    return tuple(
        (b.reshape(*filled.shape[:along], *a.shape[along:]) for a, b in zip(arrays, blocks))
    )


def spectral_axes(nf, nd):
    fidx = jnp.arange(nf, dtype=jnp.float32)
    speed = jnp.power(jnp.float32(1.1), -fidx)
    ratio = (fidx + 1.0) / nf
    didx = jnp.arange(nd, dtype=jnp.float32)
    theta = 2.0 * jnp.pi * (didx + 0.5) / nd
    psi = 2.0 * jnp.pi * (didx + 1.0) / nd
    return (speed, ratio, theta, psi)


def expander(nfreq, ndir):
    column = jnp.arange(nfreq * ndir, dtype=jnp.int32) // ndir
    return (jnp.arange(nfreq, dtype=jnp.int32)[:, None] == column[None, :]).astype(jnp.float32)


def local_step(kind, field, table, point, angle, classes, ratio, theta, psi):
    count = table.shape[0]
    nfreq = table.shape[1]
    ndir = theta.shape[0]
    spread_table = expander(nfreq, ndir)
    onehot = (classes[:, None] == jnp.arange(count, dtype=jnp.int32)[None, :]).astype(jnp.float32)
    strength = jnp.dot(onehot, table, precision=lax.Precision.HIGHEST) * point[:, None]
    wide_strength = jnp.dot(strength, spread_table, precision=lax.Precision.HIGHEST)[None, :, :]
    along = jnp.tile(jnp.cos(theta[None, :] - angle[:, None]), (1, nfreq))[None, :, :]
    spec = field
    if kind == 0:
        dpos = jnp.arange(nfreq * ndir, dtype=jnp.int32) % ndir
        turning = (
            wide_strength * jnp.tile(jnp.sin(psi[None, :] - angle[:, None]), (1, nfreq))[None, :, :]
        )
        following = jnp.where(
            dpos == ndir - 1, jnp.roll(spec, ndir - 1, axis=2), jnp.roll(spec, -1, axis=2)
        )
        faces = jnp.maximum(turning, 0.0) * spec + jnp.minimum(turning, 0.0) * following
        before = jnp.where(dpos == 0, jnp.roll(faces, 1 - ndir, axis=2), jnp.roll(faces, 1, axis=2))
        spec = spec - (faces - before)
    elif kind == 1:
        spec = spec * jnp.exp(wide_strength * jnp.maximum(along, 0.0))
    elif kind == 2:
        wide_ratio = jnp.dot(ratio[None, :], spread_table, precision=lax.Precision.HIGHEST)[
            :, None, :
        ]
        level = jnp.mean(spec, axis=2)
        spread = (level / (1.0 + level))[:, :, None]
        spec = spec / (1.0 + wide_strength * wide_ratio * (1.0 + 0.5 * along) * spread)
    else:
        spec = spec * jnp.exp(-wide_strength * (1.0 + 0.5 * along))
    return spec


def advect(field, neighbours, coefs):
    lead, points, width = field.shape
    for sub in range(ADV_STEPS):
        extended = with_halo(field, (("pts", 1),), HALO)
        flux = jnp.zeros((lead, points, width), jnp.float32)
        for n in range(len(coefs)):
            near = jnp.take(extended, neighbours[n], axis=1)
            flux = flux + (field - near) * coefs[n][None, :, :]
        field = field - flux
    return field


def full_coef(upwind_row, weight_row, angle_row, theta, wide_speed, nfreq):
    narrow = (
        upwind_row.T * weight_row[:, None] * jnp.abs(jnp.cos(theta[None, :] - angle_row[:, None]))
    )
    return jnp.tile(narrow, (1, nfreq)) * wide_speed[None, :]


def local(
    spectra,
    neighbours,
    upwind,
    edge_weight,
    edge_angle,
    depth_class,
    class_table,
    section_point,
    section_angle,
):
    nfreq = class_table.shape[2]
    ndir = upwind.shape[1]
    speed, ratio, theta, psi = spectral_axes(nfreq, ndir)
    wide_speed = jnp.dot(speed[None, :], expander(nfreq, ndir), precision=lax.Precision.HIGHEST)[0]
    coefs = []
    for n in range(upwind.shape[0]):
        coefs.append(
            full_coef(
                upwind[n].astype(jnp.float32),
                edge_weight[n],
                edge_angle[n],
                theta,
                wide_speed,
                nfreq,
            )
        )
    tables, strengths, angles = side_by_side(
        (class_table, section_point, section_angle), "section", 0, 1
    )
    field = spectra
    for kind in range(4):
        field = advect(field, neighbours, coefs)
        field = local_step(
            kind, field, tables[kind], strengths[kind], angles[kind], depth_class, ratio, theta, psi
        )
    return field


def solution(mesh):
    return jax.shard_map(
        local,
        mesh=mesh,
        in_specs=(
            P("section", "pts", None),
            P(None, "pts"),
            P(None, None, "pts"),
            P(None, "pts"),
            P(None, "pts"),
            P("pts"),
            P("section", None, None),
            P("section", "pts"),
            P("section", "pts"),
        ),
        out_specs=P("section", "pts", None),
        check_vma=False,
    )
```

profile of v0, /device:TPU:6, one launch (start us, length us, event | category | flops | bytes accessed | tf_op | source)
XLA Modules:
  0.0 199.1 jit_solution(1678659019527575702)
XLA Ops:
  1.7 3.5 %collective-permute-start = (f32[1,32,1152]{2,1,0:T(8,128)}, f32[1,32,1152]{2,1,0:T(8,128)S(1)}, u32[]{:S(2)}, u32[]{:S(2)}) collective-permute-start(f32[1,32,1152]{2,1,0:T(8,128)} %get-tuple-element.34), channel_id=1, source_target_pairs={{0,1},{1,2},{2,3},{3,4},{4,5},{5,6},{6,7},{7,8},{8,9},{9,10},{10,1... | collective-permute-start | bytes 442376 | tf_op jit(solution)/shard_map/ppermute | solution.py:17
  5.1 9.5 %collective-permute-start.1 = (f32[1,32,1152]{2,1,0:T(8,128)S(1)}, f32[1,32,1152]{2,1,0:T(8,128)}, u32[]{:S(2)}, u32[]{:S(2)}) collective-permute-start(f32[1,32,1152]{2,1,0:T(8,128)S(1)} %get-tuple-element.35), channel_id=1, source_target_pairs={{1,0},{2,1},{3,2},{4,3},{5,4},{6,5},{7,6},{8,7},{9,8},{10,9},{11,1... | collective-permute-start | bytes 442376 | tf_op jit(solution)/shard_map/ppermute | solution.py:20
  16.1 9.9 %all-gather = f32[4,1,480]{2,1,0:T(1,128)S(1)} all-gather(f32[1,1,480]{2,1,0:T(1,128)S(1)} %maximum_bitcast_fusion.8), channel_id=1, replica_groups=mesh['section'=4,'pts'=128] {'section'}, dimensions={0}, use_global_device_ids=true | all-gather | bytes 9600 | tf_op jit(solution)/shard_map/all_gather | solution.py:30
  34.1 1.7 gather_fusion
  39.1 1.8 gather_fusion.3
  41.6 1.8 fusion.104
  43.4 1.9 collective-permute-start.2
  45.4 8.7 %collective-permute-start.3 = (f32[1,32,1152]{2,1,0:T(8,128)S(1)}, f32[1,32,1152]{2,1,0:T(8,128)S(1)}, u32[]{:S(2)}, u32[]{:S(2)}) collective-permute-start(f32[1,32,1152]{2,1,0:T(8,128)S(1)} %get-tuple-element.33), channel_id=1, source_target_pairs={{1,0},{2,1},{3,2},{4,3},{5,4},{6,5},{7,6},{8,7},{9,8},{10,9},{11,1... | collective-permute-start | bytes 442376 | tf_op jit(solution)/shard_map/ppermute | solution.py:20
  58.4 1.7 gather_fusion.5
  67.3 1.9 collective-permute-start.4
  69.2 9.2 %collective-permute-start.5 = (f32[1,32,1152]{2,1,0:T(8,128)S(1)}, f32[1,32,1152]{2,1,0:T(8,128)S(1)}, u32[]{:S(2)}, u32[]{:S(2)}) collective-permute-start(f32[1,32,1152]{2,1,0:T(8,128)S(1)} %get-tuple-element.31), channel_id=1, source_target_pairs={{1,0},{2,1},{3,2},{4,3},{5,4},{6,5},{7,6},{8,7},{9,8},{10,9},{11,1... | collective-permute-start | bytes 442376 | tf_op jit(solution)/shard_map/ppermute | solution.py:20
  82.0 1.7 gather_fusion.9
  88.8 1.9 collective-permute-start.6
  90.7 9.2 %collective-permute-start.7 = (f32[1,32,1152]{2,1,0:T(8,128)S(1)}, f32[1,32,1152]{2,1,0:T(8,128)S(1)}, u32[]{:S(2)}, u32[]{:S(2)}) collective-permute-start(f32[1,32,1152]{2,1,0:T(8,128)S(1)} %get-tuple-element.29), channel_id=1, source_target_pairs={{1,0},{2,1},{3,2},{4,3},{5,4},{6,5},{7,6},{8,7},{9,8},{10,9},{11,1... | collective-permute-start | bytes 442376 | tf_op jit(solution)/shard_map/ppermute | solution.py:20
  103.5 1.7 gather_fusion.13
  106.9 1.8 gather_fusion.15
  108.7 2.1 %fusion.6 = f32[1,96,1152]{2,1,0:T(8,128)S(1)} fusion(f32[96,1152]{1,0:T(8,128)} %copy.33, f32[96,36]{0,1:T(8,128)S(1)} %copy-done.30, f32[1,96,1152]{2,1,0:T(8,128)S(1)} %fusion.80, f32[96,1152]{1,0:T(8,128)} %gather_fusion.15, f32[96,1152]{1,0:T(8,128)} %gather_fusion.14, f32[96,1152]{1,0:T(8,128)} %gather_fusion.13, f32[96,1152]{1,0:T(8,128)S(1)} %gather_fusion.12, ...), kind=kOutput, calls=%fused_computation.41 | convolution fusion | flops 50250240 | bytes 4889472 | tf_op jit(solution)/shard_map/dot_general | solution.py:59
  110.9 1.9 collective-permute-start.8
  112.8 9.4 %collective-permute-start.9 = (f32[1,32,1152]{2,1,0:T(8,128)S(1)}, f32[1,32,1152]{2,1,0:T(8,128)S(1)}, u32[]{:S(2)}, u32[]{:S(2)}) collective-permute-start(f32[1,32,1152]{2,1,0:T(8,128)S(1)} %get-tuple-element.27), channel_id=1, source_target_pairs={{1,0},{2,1},{3,2},{4,3},{5,4},{6,5},{7,6},{8,7},{9,8},{10,9},{11,1... | collective-permute-start | bytes 442376 | tf_op jit(solution)/shard_map/ppermute | solution.py:20
  129.0 1.8 gather_fusion.19
  132.5 1.9 collective-permute-start.10
  134.4 9.2 %collective-permute-start.11 = (f32[1,32,1152]{2,1,0:T(8,128)S(1)}, f32[1,32,1152]{2,1,0:T(8,128)S(1)}, u32[]{:S(2)}, u32[]{:S(2)}) collective-permute-start(f32[1,32,1152]{2,1,0:T(8,128)S(1)} %get-tuple-element.25), channel_id=1, source_target_pairs={{1,0},{2,1},{3,2},{4,3},{5,4},{6,5},{7,6},{8,7},{9,8},{10,9},{11,1... | collective-permute-start | bytes 442376 | tf_op jit(solution)/shard_map/ppermute | solution.py:20
  147.2 1.7 gather_fusion.21
  150.6 1.8 gather_fusion.23
  152.4 1.8 fusion.142
  154.8 1.9 collective-permute-start.12
  156.7 9.2 %collective-permute-start.13 = (f32[1,32,1152]{2,1,0:T(8,128)S(1)}, f32[1,32,1152]{2,1,0:T(8,128)S(1)}, u32[]{:S(2)}, u32[]{:S(2)}) collective-permute-start(f32[1,32,1152]{2,1,0:T(8,128)S(1)} %get-tuple-element.23), channel_id=1, source_target_pairs={{1,0},{2,1},{3,2},{4,3},{5,4},{6,5},{7,6},{8,7},{9,8},{10,9},{11,1... | collective-permute-start | bytes 442376 | tf_op jit(solution)/shard_map/ppermute | solution.py:20
  169.5 1.7 gather_fusion.25
  176.3 1.9 collective-permute-start.14
  178.2 9.2 %collective-permute-start.15 = (f32[1,32,1152]{2,1,0:T(8,128)S(1)}, f32[1,32,1152]{2,1,0:T(8,128)S(1)}, u32[]{:S(2)}, u32[]{:S(2)}) collective-permute-start(f32[1,32,1152]{2,1,0:T(8,128)S(1)} %get-tuple-element.21), channel_id=1, source_target_pairs={{1,0},{2,1},{3,2},{4,3},{5,4},{6,5},{7,6},{8,7},{9,8},{10,9},{11,1... | collective-permute-start | bytes 442376 | tf_op jit(solution)/shard_map/ppermute | solution.py:20
  194.4 1.8 gather_fusion.31
  196.2 2.8 %fusion.10 = f32[1,96,1152]{2,1,0:T(8,128)} fusion(f32[96,1152]{1,0:T(8,128)} %copy.35, f32[96,36]{0,1:T(8,128)S(1)} %copy-done.29, f32[1,96,1152]{2,1,0:T(8,128)S(1)} %fusion.32, f32[96,1152]{1,0:T(8,128)} %gather_fusion.31, f32[96,1152]{1,0:T(8,128)} %gather_fusion.30, f32[96,1152]{1,0:T(8,128)} %gather_fusion.29, f32[96,1152]{1,0:T(8,128)S(1)} %gather_fusion.28, ...), kind=kOutput, calls=%fused_computation.46 | convolution fusion | flops 50360832 | bytes 4889472 | tf_op jit(solution)/shard_map/dot_general | solution.py:59
  (210 shorter events, 70.2 us)
Async XLA Ops:
  1.7 30.9 %collective-permute-start = (f32[1,32,1152]{2,1,0:T(8,128)}, f32[1,32,1152]{2,1,0:T(8,128)S(1)}, u32[]{:S(2)}, u32[]{:S(2)}) collective-permute-start(f32[1,32,1152]{2,1,0:T(8,128)} %get-tuple-element.34), channel_id=1, source_target_pairs={{0,1},{1,2},{2,3},{3,4},{4,5},{5,6},{6,7},{7,8},{8,9},{9,10},{10,1... | collective-permute-start | bytes 442376 | tf_op jit(solution)/shard_map/ppermute | solution.py:17
  5.1 27.4 %collective-permute-start.1 = (f32[1,32,1152]{2,1,0:T(8,128)S(1)}, f32[1,32,1152]{2,1,0:T(8,128)}, u32[]{:S(2)}, u32[]{:S(2)}) collective-permute-start(f32[1,32,1152]{2,1,0:T(8,128)S(1)} %get-tuple-element.35), channel_id=1, source_target_pairs={{1,0},{2,1},{3,2},{4,3},{5,4},{6,5},{7,6},{8,7},{9,8},{10,9},{11,1... | collective-permute-start | bytes 442376 | tf_op jit(solution)/shard_map/ppermute | solution.py:20
  26.0 2.6 %copy-start.46 = (s32[96]{0:T(128)S(1)}, s32[96]{0:T(128)}, u32[]{:S(2)}) copy-start(s32[96]{0:T(128)} %param.16) | copy-start | bytes 1156
  26.7 2.8 %copy-start.3 = (s32[4,32,96]{2,1,0:T(8,128)S(1)}, s32[4,32,96]{2,1,0:T(8,128)}, u32[]{:S(2)}) copy-start(s32[4,32,96]{2,1,0:T(8,128)} %param.13) | copy-start | bytes 147460
  43.4 10.7 %copy-start.7 = (f32[96,32]{0,1:T(8,128)S(1)}, f32[96,32]{0,1:T(8,128)}, u32[]{:S(2)}) copy-start(f32[96,32]{0,1:T(8,128)} %get-tuple-element.73) | copy-start | bytes 36868
  43.4 12.8 %collective-permute-start.2 = (f32[1,32,1152]{2,1,0:T(8,128)S(1)}, f32[1,32,1152]{2,1,0:T(8,128)S(1)}, u32[]{:S(2)}, u32[]{:S(2)}) collective-permute-start(f32[1,32,1152]{2,1,0:T(8,128)S(1)} %get-tuple-element.32), channel_id=1, source_target_pairs={{0,1},{1,2},{2,3},{3,4},{4,5},{5,6},{6,7},{7,8},{8,9},{9,10},{10,1... | collective-permute-start | bytes 442376 | tf_op jit(solution)/shard_map/ppermute | solution.py:17
  45.4 12.1 %collective-permute-start.3 = (f32[1,32,1152]{2,1,0:T(8,128)S(1)}, f32[1,32,1152]{2,1,0:T(8,128)S(1)}, u32[]{:S(2)}, u32[]{:S(2)}) collective-permute-start(f32[1,32,1152]{2,1,0:T(8,128)S(1)} %get-tuple-element.33), channel_id=1, source_target_pairs={{1,0},{2,1},{3,2},{4,3},{5,4},{6,5},{7,6},{8,7},{9,8},{10,9},{11,1... | collective-permute-start | bytes 442376 | tf_op jit(solution)/shard_map/ppermute | solution.py:20
  67.0 11.4 %copy-start.6 = (f32[96,32]{0,1:T(8,128)S(1)}, f32[96,32]{0,1:T(8,128)}, u32[]{:S(2)}) copy-start(f32[96,32]{0,1:T(8,128)} %get-tuple-element.63) | copy-start | bytes 36868
  67.3 12.9 %collective-permute-start.4 = (f32[1,32,1152]{2,1,0:T(8,128)S(1)}, f32[1,32,1152]{2,1,0:T(8,128)S(1)}, u32[]{:S(2)}, u32[]{:S(2)}) collective-permute-start(f32[1,32,1152]{2,1,0:T(8,128)S(1)} %get-tuple-element.30), channel_id=1, source_target_pairs={{0,1},{1,2},{2,3},{3,4},{4,5},{5,6},{6,7},{7,8},{8,9},{9,10},{10,1... | collective-permute-start | bytes 442376 | tf_op jit(solution)/shard_map/ppermute | solution.py:17
  69.2 11.9 %collective-permute-start.5 = (f32[1,32,1152]{2,1,0:T(8,128)S(1)}, f32[1,32,1152]{2,1,0:T(8,128)S(1)}, u32[]{:S(2)}, u32[]{:S(2)}) collective-permute-start(f32[1,32,1152]{2,1,0:T(8,128)S(1)} %get-tuple-element.31), channel_id=1, source_target_pairs={{1,0},{2,1},{3,2},{4,3},{5,4},{6,5},{7,6},{8,7},{9,8},{10,9},{11,1... | collective-permute-start | bytes 442376 | tf_op jit(solution)/shard_map/ppermute | solution.py:20
  88.8 11.2 %copy-start.35 = (f32[8,36]{1,0:T(8,128)S(1)}, f32[8,36]{1,0:T(8,128)}, u32[]{:S(2)}) copy-start(f32[8,36]{1,0:T(8,128)} %squeeze.21) | copy-start | bytes 3460
  88.8 12.3 %collective-permute-start.6 = (f32[1,32,1152]{2,1,0:T(8,128)S(1)}, f32[1,32,1152]{2,1,0:T(8,128)S(1)}, u32[]{:S(2)}, u32[]{:S(2)}) collective-permute-start(f32[1,32,1152]{2,1,0:T(8,128)S(1)} %get-tuple-element.28), channel_id=1, source_target_pairs={{0,1},{1,2},{2,3},{3,4},{4,5},{5,6},{6,7},{7,8},{8,9},{9,10},{10,1... | collective-permute-start | bytes 442376 | tf_op jit(solution)/shard_map/ppermute | solution.py:17
  90.7 9.2 %copy-start.45 = (f32[96]{0:T(128)S(1)}, f32[96]{0:T(128)}, u32[]{:S(2)}) copy-start(f32[96]{0:T(128)} %get-tuple-element.43) | copy-start | bytes 1156
  90.7 9.2 %copy-start.47 = (s32[96]{0:T(128)S(1)}, s32[96]{0:T(128)}, u32[]{:S(2)}) copy-start(s32[96]{0:T(128)} %param.16) | copy-start | bytes 1156
  90.7 11.8 %collective-permute-start.7 = (f32[1,32,1152]{2,1,0:T(8,128)S(1)}, f32[1,32,1152]{2,1,0:T(8,128)S(1)}, u32[]{:S(2)}, u32[]{:S(2)}) collective-permute-start(f32[1,32,1152]{2,1,0:T(8,128)S(1)} %get-tuple-element.29), channel_id=1, source_target_pairs={{1,0},{2,1},{3,2},{4,3},{5,4},{6,5},{7,6},{8,7},{9,8},{10,9},{11,1... | collective-permute-start | bytes 442376 | tf_op jit(solution)/shard_map/ppermute | solution.py:20
  110.9 11.3 %copy-start.32 = (f32[288]{0:T(512)S(1)}, f32[288]{0:T(512)}, u32[]{:S(2)}) copy-start(f32[288]{0:T(512)} %get-tuple-element.6) | copy-start | bytes 3460
  110.9 12.3 %collective-permute-start.8 = (f32[1,32,1152]{2,1,0:T(8,128)S(1)}, f32[1,32,1152]{2,1,0:T(8,128)S(1)}, u32[]{:S(2)}, u32[]{:S(2)}) collective-permute-start(f32[1,32,1152]{2,1,0:T(8,128)S(1)} %get-tuple-element.26), channel_id=1, source_target_pairs={{0,1},{1,2},{2,3},{3,4},{4,5},{5,6},{6,7},{7,8},{8,9},{9,10},{10,1... | collective-permute-start | bytes 442376 | tf_op jit(solution)/shard_map/ppermute | solution.py:17
  112.8 11.8 %collective-permute-start.9 = (f32[1,32,1152]{2,1,0:T(8,128)S(1)}, f32[1,32,1152]{2,1,0:T(8,128)S(1)}, u32[]{:S(2)}, u32[]{:S(2)}) collective-permute-start(f32[1,32,1152]{2,1,0:T(8,128)S(1)} %get-tuple-element.27), channel_id=1, source_target_pairs={{1,0},{2,1},{3,2},{4,3},{5,4},{6,5},{7,6},{8,7},{9,8},{10,9},{11,1... | collective-permute-start | bytes 442376 | tf_op jit(solution)/shard_map/ppermute | solution.py:20
  132.5 11.2 %copy-start.36 = (f32[8,36]{1,0:T(8,128)S(1)}, f32[8,36]{1,0:T(8,128)}, u32[]{:S(2)}) copy-start(f32[8,36]{1,0:T(8,128)} %squeeze.22) | copy-start | bytes 3460
  132.5 13.1 %collective-permute-start.10 = (f32[1,32,1152]{2,1,0:T(8,128)S(1)}, f32[1,32,1152]{2,1,0:T(8,128)S(1)}, u32[]{:S(2)}, u32[]{:S(2)}) collective-permute-start(f32[1,32,1152]{2,1,0:T(8,128)S(1)} %get-tuple-element.24), channel_id=1, source_target_pairs={{0,1},{1,2},{2,3},{3,4},{4,5},{5,6},{6,7},{7,8},{8,9},{9,10},{10,1... | collective-permute-start | bytes 442376 | tf_op jit(solution)/shard_map/ppermute | solution.py:17
  134.4 9.2 %copy-start.44 = (f32[96]{0:T(128)S(1)}, f32[96]{0:T(128)}, u32[]{:S(2)}) copy-start(f32[96]{0:T(128)} %get-tuple-element.40) | copy-start | bytes 1156
  134.4 9.2 %copy-start.48 = (s32[96]{0:T(128)S(1)}, s32[96]{0:T(128)}, u32[]{:S(2)}) copy-start(s32[96]{0:T(128)} %param.16) | copy-start | bytes 1156
  134.4 11.8 %collective-permute-start.11 = (f32[1,32,1152]{2,1,0:T(8,128)S(1)}, f32[1,32,1152]{2,1,0:T(8,128)S(1)}, u32[]{:S(2)}, u32[]{:S(2)}) collective-permute-start(f32[1,32,1152]{2,1,0:T(8,128)S(1)} %get-tuple-element.25), channel_id=1, source_target_pairs={{1,0},{2,1},{3,2},{4,3},{5,4},{6,5},{7,6},{8,7},{9,8},{10,9},{11,1... | collective-permute-start | bytes 442376 | tf_op jit(solution)/shard_map/ppermute | solution.py:20
  152.4 1.9 copy-start.2
  154.3 11.6 %copy-start.4 = (f32[96,32]{0,1:T(8,128)S(1)}, f32[96,32]{0,1:T(8,128)}, u32[]{:S(2)}) copy-start(f32[96,32]{0,1:T(8,128)} %get-tuple-element.64) | copy-start | bytes 36868
  154.8 12.9 %collective-permute-start.12 = (f32[1,32,1152]{2,1,0:T(8,128)S(1)}, f32[1,32,1152]{2,1,0:T(8,128)S(1)}, u32[]{:S(2)}, u32[]{:S(2)}) collective-permute-start(f32[1,32,1152]{2,1,0:T(8,128)S(1)} %get-tuple-element.22), channel_id=1, source_target_pairs={{0,1},{1,2},{2,3},{3,4},{4,5},{5,6},{6,7},{7,8},{8,9},{9,10},{10,1... | collective-permute-start | bytes 442376 | tf_op jit(solution)/shard_map/ppermute | solution.py:17
  156.7 11.8 %collective-permute-start.13 = (f32[1,32,1152]{2,1,0:T(8,128)S(1)}, f32[1,32,1152]{2,1,0:T(8,128)S(1)}, u32[]{:S(2)}, u32[]{:S(2)}) collective-permute-start(f32[1,32,1152]{2,1,0:T(8,128)S(1)} %get-tuple-element.23), channel_id=1, source_target_pairs={{1,0},{2,1},{3,2},{4,3},{5,4},{6,5},{7,6},{8,7},{9,8},{10,9},{11,1... | collective-permute-start | bytes 442376 | tf_op jit(solution)/shard_map/ppermute | solution.py:20
  176.3 11.2 %copy-start.34 = (f32[8,36]{1,0:T(8,128)S(1)}, f32[8,36]{1,0:T(8,128)}, u32[]{:S(2)}) copy-start(f32[8,36]{1,0:T(8,128)} %squeeze.23) | copy-start | bytes 3460
  176.3 12.3 %collective-permute-start.14 = (f32[1,32,1152]{2,1,0:T(8,128)S(1)}, f32[1,32,1152]{2,1,0:T(8,128)S(1)}, u32[]{:S(2)}, u32[]{:S(2)}) collective-permute-start(f32[1,32,1152]{2,1,0:T(8,128)S(1)} %get-tuple-element.20), channel_id=1, source_target_pairs={{0,1},{1,2},{2,3},{3,4},{4,5},{5,6},{6,7},{7,8},{8,9},{9,10},{10,1... | collective-permute-start | bytes 442376 | tf_op jit(solution)/shard_map/ppermute | solution.py:17
  178.2 9.2 %copy-start.43 = (f32[96]{0:T(128)S(1)}, f32[96]{0:T(128)}, u32[]{:S(2)}) copy-start(f32[96]{0:T(128)} %get-tuple-element.44) | copy-start | bytes 1156
  178.2 9.2 %copy-start.49 = (s32[96]{0:T(128)S(1)}, s32[96]{0:T(128)}, u32[]{:S(2)}) copy-start(s32[96]{0:T(128)} %param.16) | copy-start | bytes 1156
  178.2 11.8 %collective-permute-start.15 = (f32[1,32,1152]{2,1,0:T(8,128)S(1)}, f32[1,32,1152]{2,1,0:T(8,128)S(1)}, u32[]{:S(2)}, u32[]{:S(2)}) collective-permute-start(f32[1,32,1152]{2,1,0:T(8,128)S(1)} %get-tuple-element.21), channel_id=1, source_target_pairs={{1,0},{2,1},{3,2},{4,3},{5,4},{6,5},{7,6},{8,7},{9,8},{10,9},{11,1... | collective-permute-start | bytes 442376 | tf_op jit(solution)/shard_map/ppermute | solution.py:20
  (34 other events, 48.3 us)
where the time goes:
time: 201 us; the launch traced here: 199 us
  starting transfers between devices  90.4 us (45%)
  local copies, waits for them, and re-layouts  64 us (32%)
  other arithmetic  14.8 us (7%)
  waiting for transfers between devices  10 us (5%)
  blocking collectives  9.86 us (5%)
  matrix products  9.05 us (5%)
    ppermute x8, starting transfers between devices, with_halo(): lax.ppermute(lax.slice_in_dim(block, 0, width, axis=dim), axis, backward)  73.5 us
    gather x32, local copies, waits for them, and re-layouts, advect(): near = jnp.take(extended, neighbours[n], axis=1)  48.9 us
    ppermute x8, starting transfers between devices, with_halo(): lax.ppermute(lax.slice_in_dim(block, block.shape[dim] - width, None, axis...  16.9 us
    all_gather x1, blocking collectives, side_by_side(): filled = lax.all_gather(both, axis, axis=dim, tiled=True)  9.86 us
    sub x5, other arithmetic, advect(): field = field - flux  8.41 us
    ppermute x8, waiting for transfers between devices, with_halo(): lax.ppermute(lax.slice_in_dim(block, 0, width, axis=dim), axis, backward)  8.08 us
    dot_general x4, matrix products, local_step(): jnp.dot(strength, spread_table, precision=lax.Precision.HIGHEST)[None, :, :]  5.86 us
  transfers between devices with their start and end apart: 16, of which 11 were waited for; matrix products, arithmetic and copies ran while one was open for 8% of the time, Pallas kernels for 0%

commit v1 on v0

v1 whole, which is shorter than its diff:
```python
import functools
import math

import jax
import jax.numpy as jnp
import numpy as np
from jax import lax
from jax.experimental import pallas as pl
from jax.experimental.pallas import tpu as pltpu
from jax.sharding import PartitionSpec as P

HALO = 32
LANES = 128
MESH = pl.DeviceIdType.MESH
F32 = jnp.float32
BF16 = jnp.bfloat16


def constant_rows(nf, nd, chunks):
    lane = np.arange(LANES)
    theta = 2.0 * np.pi * (np.arange(nd) + 0.5) / nd
    psi = 2.0 * np.pi * (np.arange(nd) + 1.0) / nd
    speed = 1.1 ** -np.arange(nf, dtype=np.float64)
    ratio = (np.arange(nf) + 1.0) / nf
    per = LANES // nd
    rows = [np.cos(theta)[lane % nd], np.sin(theta)[lane % nd], np.cos(psi)[lane % nd], np.sin(psi)[lane % nd]]
    rows += [np.zeros(LANES)] * 4
    rows += [speed[c * per + lane // nd] for c in range(chunks)]
    rows += [ratio[c * per + lane // nd] for c in range(chunks)]
    while len(rows) % 8:
        rows.append(np.zeros(LANES))
    base = len(rows)
    rows += [np.full(LANES, v) for v in np.cos(theta)]
    rows += [np.full(LANES, v) for v in np.sin(theta)]
    return np.stack(rows).astype(np.float32), base


def split2(x):
    hi = x.astype(BF16)
    lo = (x - hi.astype(F32)).astype(BF16)
    return hi, lo


def kernel(
    geo, spec, nbr, upw, wgt, ang, cls, tab, pnt, sang, consts, out,
    ext, outv, nbr_v, upw_v, wgt_v, ang_v, cls_v, tab_v, pnt_v, sang_v, pnt_h, sang_h, con,
    cown, chalo, tbuf, ttr, cf, csum, oh1, oh2, ohc, tw, dir3, dir2, h2, x3,
    load_sem, small_sem, send_sem, recv_sem, meta_send, meta_recv, sec_send, sec_recv, out_sem,
):
    n_pts, n_sec, points, nd, nb, nc, nf, chunks, base = geo
    two = 2 * HALO
    wide = points + 2 * two
    mid = points + 2 * HALO
    t = lax.axis_index("pts")
    s = lax.axis_index("section")
    has_l = t > 0
    has_r = t < n_pts - 1
    sides = ((has_l, {"pts": t - 1}), (has_r, {"pts": t + 1}))

    barrier = pltpu.get_barrier_semaphore()
    for there, dev in sides:
        @pl.when(there)
        def _():
            pl.semaphore_signal(barrier, inc=1, device_id=dev, device_id_type=MESH)
    for o in range(1, n_sec):
        pl.semaphore_signal(
            barrier, inc=1, device_id={"section": lax.rem(s + o, n_sec)}, device_id_type=MESH
        )

    small = [
        pltpu.make_async_copy(upw, upw_v, small_sem.at[0]),
        pltpu.make_async_copy(consts, con, small_sem.at[1]),
        pltpu.make_async_copy(wgt, wgt_v, small_sem.at[2]),
        pltpu.make_async_copy(ang, ang_v, small_sem.at[3]),
        pltpu.make_async_copy(nbr, nbr_v.at[0], small_sem.at[4]),
        pltpu.make_async_copy(cls, cls_v.at[0], small_sem.at[5]),
        pltpu.make_async_copy(tab.at[0], tab_v.at[s], small_sem.at[6]),
        pltpu.make_async_copy(pnt, pnt_v.at[s], small_sem.at[7]),
        pltpu.make_async_copy(sang, sang_v.at[s], small_sem.at[8]),
    ]
    for cp in small:
        cp.start()
    loads = [
        pltpu.make_async_copy(
            spec.at[0, :, pl.ds(c * LANES, LANES)], ext.at[0, c, pl.ds(two, points)], load_sem.at[c]
        )
        for c in range(chunks)
    ]
    for cp in loads:
        cp.start()

    for side, (there, _) in enumerate(sides):
        @pl.when(jnp.logical_not(there))
        def _():
            lo = 0 if side == 0 else two + points
            for e in range(4):
                for c in range(chunks):
                    ext[e, c, pl.ds(lo, two)] = jnp.zeros((two, LANES), F32)
            nbr_v[1 + side] = jnp.zeros((nb, points), jnp.int32)
            cls_v[1 + side] = jnp.zeros((1, points), jnp.int32)
            pnt_h[side] = jnp.zeros((1, points), F32)
            sang_h[side] = jnp.zeros((1, points), F32)
            chalo[side] = jnp.zeros((HALO, LANES), F32)

    for cp in small:
        cp.wait()

    cos_d = con[pl.ds(base, nd), pl.ds(0, points)]
    sin_d = con[pl.ds(base + nd, nd), pl.ds(0, points)]
    cos_e = jnp.cos(ang_v[...])
    sin_e = jnp.sin(ang_v[...])
    for n in range(nb):
        along = jnp.abs(cos_d * cos_e[n : n + 1] + sin_d * sin_e[n : n + 1])
        tbuf[pl.ds(n * nd, nd), pl.ds(0, points)] = upw_v[n].astype(F32) * wgt_v[n : n + 1, :] * along
    cown[...] = jnp.transpose(tbuf[...])[0:points]

    pl.semaphore_wait(barrier, n_sec - 1 + has_l.astype(jnp.int32) + has_r.astype(jnp.int32))

    def remote(src, dst, ssem, rsem, dev):
        return pltpu.make_async_remote_copy(
            src_ref=src, dst_ref=dst, send_sem=ssem, recv_sem=rsem, device_id=dev, device_id_type=MESH
        )

    def meta(side):
        dev = sides[side][1]
        far = 1 - side
        rows = pl.ds(0, HALO) if side == 0 else pl.ds(points - HALO, HALO)
        return [
            remote(nbr_v.at[0], nbr_v.at[1 + far], meta_send.at[side, 0], meta_recv.at[far, 0], dev),
            remote(cown.at[rows], chalo.at[far], meta_send.at[side, 1], meta_recv.at[far, 1], dev),
            remote(cls_v.at[0], cls_v.at[1 + far], meta_send.at[side, 2], meta_recv.at[far, 2], dev),
            remote(pnt_v.at[2], pnt_h.at[far], meta_send.at[side, 3], meta_recv.at[far, 3], dev),
            remote(sang_v.at[2], sang_h.at[far], meta_send.at[side, 4], meta_recv.at[far, 4], dev),
        ]

    def halo(e, c, side):
        dev = sides[side][1]
        far = 1 - side
        src = pl.ds(two, two) if side == 0 else pl.ds(points, two)
        dst = pl.ds(two + points, two) if side == 0 else pl.ds(0, two)
        return remote(
            ext.at[e, c, src], ext.at[e, c, dst], send_sem.at[e, side, c], recv_sem.at[e, far, c], dev
        )

    def arrival(e, c, side):
        dev = sides[side][1]
        dst = pl.ds(0, two) if side == 0 else pl.ds(two + points, two)
        return remote(
            ext.at[e, c, dst], ext.at[e, c, dst], send_sem.at[e, side, c], recv_sem.at[e, side, c], dev
        )

    def meta_arrival(side, k):
        dev = sides[side][1]
        ref = (nbr_v.at[1 + side], chalo.at[side], cls_v.at[1 + side], pnt_h.at[side], sang_h.at[side])[k]
        return remote(ref, ref, meta_send.at[side, k], meta_recv.at[side, k], dev)

    def sections(o):
        dev = {"section": lax.rem(s + o, n_sec)}
        return [
            remote(ref.at[s], ref.at[s], sec_send.at[o - 1, k], sec_recv.at[o - 1, k], dev)
            for k, ref in enumerate((tab_v, pnt_v, sang_v))
        ]

    for side, (there, _) in enumerate(sides):
        @pl.when(there)
        def _():
            for cp in meta(side)[:3]:
                cp.start()
    for o in range(1, n_sec):
        for cp in sections(o):
            cp.start()
    for c in range(chunks):
        loads[c].wait()
        for side, (there, _) in enumerate(sides):
            @pl.when(there)
            def _():
                halo(0, c, side).start()

    for side, (there, _) in enumerate(sides):
        @pl.when(there)
        def _():
            for k in range(3):
                meta_arrival(side, k).wait_recv()
    for k in range(3):
        tbuf[pl.ds(k * nb, nb), pl.ds(0, points)] = nbr_v[k].astype(F32)
    cols = jnp.transpose(tbuf[...])
    col_id = lax.broadcasted_iota(jnp.int32, (mid, 2 * LANES), 1).astype(F32)
    for n in range(nb):
        own = cols[0:points, n : n + 1]
        left = cols[points - HALO : points, nb + n : nb + n + 1]
        right = cols[0:HALO, 2 * nb + n : 2 * nb + n + 1]
        at1 = jnp.concatenate([left - two, own + HALO, right + (points + HALO)], axis=0)
        oh1[pl.ds(n * mid, mid)] = (col_id == at1).astype(F32).astype(BF16)
        oh2[pl.ds(n * points, points)] = (col_id[0:points] == own).astype(F32).astype(BF16)
    narrow = jnp.concatenate([chalo[0], cown[...], chalo[1]], axis=0)
    lane = lax.broadcasted_iota(jnp.int32, (mid, LANES), 1)
    total = jnp.zeros((mid, LANES), F32)
    for n in range(nb):
        only = jnp.where(lane // nd == n, narrow, 0.0)
        step = nd
        while step < LANES:
            only = only + pltpu.roll(only, step, 1)
            step *= 2
        cf[n] = only
        total = total + only
    csum[...] = total

    for o in range(1, n_sec):
        for cp in sections(o):
            cp.wait_recv()
    for side, (there, _) in enumerate(sides):
        @pl.when(there)
        def _():
            for cp in meta(side)[3:]:
                cp.start()
    for k in range(n_sec):
        tbuf[pl.ds(k, 1), pl.ds(0, points)] = pnt_v[k]
        phi = sang_v[k]
        tbuf[pl.ds(8 + k, 1), pl.ds(0, points)] = jnp.cos(phi)
        tbuf[pl.ds(16 + k, 1), pl.ds(0, points)] = jnp.sin(phi)
    for k in range(3):
        tbuf[pl.ds(24 + k, 1), pl.ds(0, points)] = cls_v[k].astype(F32)
    ttr[...] = jnp.transpose(tbuf[...])
    cos_t, sin_t = con[0:1], con[1:2]
    cos_p, sin_p = con[2:3], con[3:4]

    def column(k, rows=(0, points)):
        return ttr[rows[0] : rows[1], k : k + 1]

    dir3[0] = column(0) * (sin_p * column(8) - cos_p * column(16))
    dir3[1] = column(1) * jnp.maximum(cos_t * column(9) + sin_t * column(17), 0.0)
    dir3[2] = column(3) * (1.0 + 0.5 * (cos_t * column(11) + sin_t * column(19)))
    dir2[pl.ds(two, points)] = column(2) * (1.0 + 0.5 * (cos_t * column(10) + sin_t * column(18)))

    expand = (
        lax.broadcasted_iota(jnp.int32, (nf, nf * nd), 0)
        == lax.broadcasted_iota(jnp.int32, (nf, nf * nd), 1) // nd
    ).astype(F32).astype(BF16)
    for k in range(n_sec):
        table = tab_v[k]
        hi = table.astype(BF16).astype(F32)
        md = (table - hi).astype(BF16).astype(F32)
        lo = table - hi - md
        parts = jnp.concatenate([hi, md, lo], axis=0).astype(BF16)
        spread_out = jnp.dot(parts, expand, preferred_element_type=F32)
        for c in range(chunks):
            tw[k, c] = spread_out[:, c * LANES : (c + 1) * LANES].astype(BF16)
    kid = lax.broadcasted_iota(jnp.int32, (wide, 3 * nc), 1) % nc
    classes = jnp.concatenate(
        [column(25, (points - two, points)), column(24), column(26, (0, two))], axis=0
    )
    ohc[...] = (kid.astype(F32) == classes).astype(F32).astype(BF16)

    def strength(k, c, rows):
        return jnp.dot(ohc[rows], tw[k, c], preferred_element_type=F32)

    own_rows = pl.ds(two, points)

    def gathered(onehot, field, rows):
        depth = field.shape[0]
        hi, lo = split2(field)
        rhs = jnp.concatenate([hi, lo], axis=1)
        if depth < 2 * LANES:
            rhs = jnp.concatenate([rhs, jnp.zeros((2 * LANES - depth, 2 * LANES), BF16)], axis=0)
        res = jnp.dot(onehot, rhs, preferred_element_type=F32)
        near = res[:, :LANES] + res[:, LANES:]
        return [near[n * rows : (n + 1) * rows] for n in range(nb)]

    def advect_twice(field, c):
        speed = con[pl.ds(8 + c, 1), :]
        near = gathered(oh1[...], field, mid)
        flux = near[0] * cf[0]
        for n in range(1, nb):
            flux = flux + near[n] * cf[n]
        first = field[HALO : HALO + mid] * (1.0 - speed * csum[...]) + speed * flux
        near = gathered(oh2[...], first, points)
        inner = pl.ds(HALO, points)
        flux = near[0] * cf[0, inner]
        for n in range(1, nb):
            flux = flux + near[n] * cf[n, inner]
        return first[HALO : HALO + points] * (1.0 - speed * csum[inner]) + speed * flux

    lane_own = lax.broadcasted_iota(jnp.int32, (points, LANES), 1) % nd

    def wait_halo(e, c):
        for side, (there, _) in enumerate(sides):
            @pl.when(there)
            def _():
                arrival(e, c, side).wait_recv()

    def hand_on(e, c, value):
        ext[e + 1, c, own_rows] = value
        for side, (there, _) in enumerate(sides):
            @pl.when(there)
            def _():
                halo(e + 1, c, side).start()

    def section0(c, carry):
        wait_halo(0, c)
        field = advect_twice(ext[0, c], c)
        turning = strength(0, c, own_rows) * dir3[0]
        following = jnp.where(
            lane_own == nd - 1, pltpu.roll(field, nd - 1, 1), pltpu.roll(field, LANES - 1, 1)
        )
        faces = jnp.maximum(turning, 0.0) * field + jnp.minimum(turning, 0.0) * following
        before = jnp.where(
            lane_own == 0, pltpu.roll(faces, LANES - nd + 1, 1), pltpu.roll(faces, 1, 1)
        )
        hand_on(0, c, field - (faces - before))
        return carry

    def section1(c, carry):
        wait_halo(1, c)
        field = advect_twice(ext[1, c], c)
        hand_on(1, c, field * jnp.exp(strength(1, c, own_rows) * dir3[1]))
        return carry

    def section2(c, carry):
        ratio = con[pl.ds(8 + chunks + c, 1), :]
        h2[c] = strength(2, c, pl.ds(0, wide)) * dir2[...] * ratio
        x3[c] = jnp.exp(-(strength(3, c, own_rows) * dir3[2]))
        wait_halo(2, c)
        hand_on(2, c, advect_twice(ext[2, c], c))
        return carry

    lax.fori_loop(0, chunks, section0, 0)
    lax.fori_loop(0, chunks, section1, 0)

    for side, (there, _) in enumerate(sides):
        @pl.when(there)
        def _():
            for k in (3, 4):
                meta_arrival(side, k).wait_recv()
    for side in range(2):
        tbuf[pl.ds(side, 1), pl.ds(0, points)] = pnt_h[side]
        tbuf[pl.ds(8 + side, 1), pl.ds(0, points)] = jnp.cos(sang_h[side])
        tbuf[pl.ds(16 + side, 1), pl.ds(0, points)] = jnp.sin(sang_h[side])
    ttr[...] = jnp.transpose(tbuf[...])
    for side in range(2):
        rows = (points - two, points) if side == 0 else (0, two)
        lo = 0 if side == 0 else two + points
        dir2[pl.ds(lo, two)] = column(side, rows) * (
            1.0 + 0.5 * (cos_t * column(8 + side, rows) + sin_t * column(16 + side, rows))
        )

    lax.fori_loop(0, chunks, section2, 0)

    def add_up(c, acc):
        wait_halo(3, c)
        return acc + ext[3, c]

    acc = lax.fori_loop(0, chunks, add_up, jnp.zeros((wide, LANES), F32))
    level = jnp.sum(acc, axis=1, keepdims=True) * (1.0 / (nf * nd))
    csum_w = jnp.broadcast_to(level / (1.0 + level), (wide, LANES))
    dir2[...] = csum_w

    def result(c):
        return pltpu.make_async_copy(
            outv.at[c], out.at[0, :, pl.ds(pl.multiple_of(c * LANES, LANES), LANES)], out_sem.at[c]
        )

    def section3(c, carry):
        field = ext[3, c] / (1.0 + h2[c] * dir2[...])
        outv[c] = advect_twice(field, c) * x3[c]
        result(c).start()
        return carry

    lax.fori_loop(0, chunks, section3, 0)

    for side, (there, _) in enumerate(sides):
        @pl.when(there)
        def _():
            for cp in meta(side):
                cp.wait_send()

            def drain(c, carry):
                for e in range(4):
                    halo(e, c, side).wait_send()
                return carry

            lax.fori_loop(0, chunks, drain, 0)
    for o in range(1, n_sec):
        for cp in sections(o):
            cp.wait_send()

    def finish(c, carry):
        result(c).wait()
        return carry

    lax.fori_loop(0, chunks, finish, 0)


def local(n_pts, n_sec, spectra, neighbours, upwind, edge_weight, edge_angle, depth_class, class_table,
          section_point, section_angle):
    points, width = spectra.shape[1:]
    nb, nd = upwind.shape[:2]
    nc, nf = class_table.shape[1:]
    chunks = width // LANES
    rows, base = constant_rows(nf, nd, chunks)
    geo = (n_pts, n_sec, points, nd, nb, nc, nf, chunks, base)
    two = 2 * HALO
    wide = points + 2 * two
    mid = points + 2 * HALO
    hbm = pl.BlockSpec(memory_space=pltpu.HBM)
    dma = pltpu.SemaphoreType.DMA
    vmem = pltpu.VMEM
    i32 = jnp.int32
    return pl.pallas_call(
        functools.partial(kernel, geo),
        name="wave_window",
        out_shape=jax.ShapeDtypeStruct((1, points, width), F32),
        in_specs=[hbm] * 10,
        out_specs=hbm,
        scratch_shapes=[
            vmem((4, chunks, wide, LANES), F32),
            vmem((chunks, points, LANES), F32),
            vmem((3, nb, points), i32),
            vmem((nb, nd, points), i32),
            vmem((nb, points), F32),
            vmem((nb, points), F32),
            vmem((3, 1, points), i32),
            vmem((n_sec, nc, nf), F32),
            vmem((n_sec, 1, points), F32),
            vmem((n_sec, 1, points), F32),
            vmem((2, 1, points), F32),
            vmem((2, 1, points), F32),
            vmem(rows.shape, F32),
            vmem((points, LANES), F32),
            vmem((2, HALO, LANES), F32),
            vmem((LANES, LANES), F32),
            vmem((LANES, LANES), F32),
            vmem((nb, mid, LANES), F32),
            vmem((mid, LANES), F32),
            vmem((nb * mid, 2 * LANES), BF16),
            vmem((nb * points, 2 * LANES), BF16),
            vmem((wide, 3 * nc), BF16),
            vmem((n_sec, chunks, 3 * nc, LANES), BF16),
            vmem((3, points, LANES), F32),
            vmem((wide, LANES), F32),
            vmem((chunks, wide, LANES), F32),
            vmem((chunks, points, LANES), F32),
            dma((chunks,)),
            dma((9,)),
            dma((4, 2, chunks)),
            dma((4, 2, chunks)),
            dma((2, 5)),
            dma((2, 5)),
            dma((n_sec - 1, 3)),
            dma((n_sec - 1, 3)),
            dma((chunks,)),
        ],
        compiler_params=pltpu.CompilerParams(
            collective_id=0, has_side_effects=True, vmem_limit_bytes=64_000_000
        ),
    )(
        spectra, neighbours, upwind, edge_weight, edge_angle, depth_class.reshape(1, points), class_table,
        section_point, section_angle, jnp.asarray(rows),
    )


def solution(mesh):
    n_pts, n_sec = mesh.shape["pts"], mesh.shape["section"]
    return jax.shard_map(
        functools.partial(local, n_pts, n_sec),
        mesh=mesh,
        in_specs=(
            P("section", "pts", None),
            P(None, "pts"),
            P(None, None, "pts"),
            P(None, "pts"),
            P(None, "pts"),
            P("pts"),
            P("section", None, None),
            P("section", "pts"),
            P("section", "pts"),
        ),
        out_specs=P("section", "pts", None),
        check_vma=False,
    )
```

time: 201 us -> 56.2 us (0.28)
  starting transfers between devices: 90.4 us -> 0 us
  local copies, waits for them, and re-layouts: 64 us -> 1.8 us
  Pallas kernels: 0 us -> 54.2 us
  other arithmetic: 14.8 us -> 0 us
  waiting for transfers between devices: 10 us -> 0 us
  blocking collectives: 9.86 us -> 0 us
  matrix products: 9.05 us -> 0 us
    ppermute x16 -> x0, starting transfers between devices: 90.4 us -> none  [the longest x8 73.5 us: with_halo(): lax.ppermute(lax.slice_in_dim(block, 0, width, axis=dim), axis, backward)]
    pallas_call x0 -> x1, Pallas kernels: none -> 54.2 us  [local(): pl.pallas_call(functools.partial(kernel, geo), name='wave_window', out_sh...]
    gather x32 -> x0, local copies, waits for them, and re-layouts: 48.9 us -> none  [advect(): near = jnp.take(extended, neighbours[n], axis=1)]
    ppermute x16 -> x0, waiting for transfers between devices: 10 us -> none  [the longest x8 8.08 us: with_halo(): lax.ppermute(lax.slice_in_dim(block, 0, width, axis=dim), axis, backward)]
    all_gather x1 -> x0, blocking collectives: 9.86 us -> none  [side_by_side(): filled = lax.all_gather(both, axis, axis=dim, tiled=True)]
    dot_general x10 -> x0, matrix products: 9.05 us -> none  [the longest x4 5.86 us: local_step(): jnp.dot(strength, spread_table, precision=lax.Precision.HIGHEST)[None, :, :]]
    sub x6 -> x0, other arithmetic: 8.63 us -> none  [the longest x5 8.41 us: advect(): field = field - flux]
    slice x12 -> x0, local copies, waits for them, and re-layouts: 2.69 us -> none  [the longest x8 1.81 us: with_halo(): lax.slice_in_dim(block, block.shape[dim] - width, None, axis=dim)]
  transfers between devices with their start and end apart: 16 -> 0, of which waited for: 11 -> 0; matrix products, arithmetic and copies ran while one was open for 8% -> 0% of each run, Pallas kernels for 0% -> 0%
where the time goes in v1:
time: 56.2 us; the launch traced here: 56 us
  Pallas kernels  54.2 us (96%)
  local copies, waits for them, and re-layouts  1.8 us (3%)
    pallas_call x1, Pallas kernels, local(): pl.pallas_call(functools.partial(kernel, geo), name='wave_window', out_sh...  54.2 us
    unnamed x1, local copies, waits for them, and re-layouts  1.8 us

profile of v1, /device:TPU:6, one launch (start us, length us, event | category | flops | bytes accessed | tf_op | source)
XLA Modules:
  0.0 56.0 jit_solution(2142704427956007324)
XLA Ops:
  0.0 54.2 %wave_window.1 = f32[1,96,1152]{2,1,0:T(8,128)} custom-call(f32[1,96,1152]{2,1,0:T(8,128)} %spec.1, s32[4,96]{1,0:T(4,128)} %nbr.1, s32[4,32,96]{2,1,0:T(8,128)} %upw.1, f32[4,96]{1,0:T(4,128)} %wgt.1, f32[4,96]{1,0:T(4,128)} %ang.1, s32[1,96]{1,0:T(1,128)} %bitcast.1, f32[1,8,36]{2,1,0:T(8,128)} %tab.1, f32[1,96]{1,0:T(1,128)} %pnt.1, f32[1,96]{1,0:T(1,128)} %sang.1, ...), custom_call_target="tpu_custom_call" | custom-call | tf_op jit(solution)/shard_map/wave_window/pallas_call | solution.py:408
  54.2 1.8 %copy.12 = f32[1,96,1152]{2,1,0:T(8,128)} copy(f32[1,96,1152]{2,1,0:T(8,128)} %wave_window.1) | data formatting | bytes 884736

commit v2 on v1

--- a/solution.py
+++ b/solution.py
@@ -11,6 +11,9 @@
 
 HALO = 32
 LANES = 128
+GROUP = 9
+ROW = 8
+PLANE = 32
 MESH = pl.DeviceIdType.MESH
 F32 = jnp.float32
 BF16 = jnp.bfloat16
@@ -43,12 +46,13 @@
 
 def kernel(
     geo, spec, nbr, upw, wgt, ang, cls, tab, pnt, sang, consts, out,
-    ext, outv, nbr_v, upw_v, wgt_v, ang_v, cls_v, tab_v, pnt_v, sang_v, pnt_h, sang_h, con,
-    cown, chalo, tbuf, ttr, cf, csum, oh1, oh2, ohc, tw, dir3, dir2, h2, x3,
+    ext0, ext, outv, fields6, fields7, total, nbr_v, upw_v, wgt_v, ang_v, cls_v, tab_v, pnt_v, sang_v, pnt_h, sang_h, con,
+    cown, chalo, tbuf, ttr, cf, csum, oh1, oh2, oh3, ohc, tw, dir3, dir1, dir2, h2, x3,
     load_sem, small_sem, send_sem, recv_sem, meta_send, meta_recv, sec_send, sec_recv, out_sem,
 ):
     n_pts, n_sec, points, nd, nb, nc, nf, chunks, base = geo
     two = 2 * HALO
+    full = points + 6 * HALO
     wide = points + 2 * two
     mid = points + 2 * HALO
     t = lax.axis_index("pts")
@@ -82,7 +86,7 @@
         cp.start()
     loads = [
         pltpu.make_async_copy(
-            spec.at[0, :, pl.ds(c * LANES, LANES)], ext.at[0, c, pl.ds(two, points)], load_sem.at[c]
+            spec.at[0, :, pl.ds(c * LANES, LANES)], ext0.at[c, pl.ds(two, points)], load_sem.at[c]
         )
         for c in range(chunks)
     ]
@@ -93,14 +97,16 @@
         @pl.when(jnp.logical_not(there))
         def _():
             lo = 0 if side == 0 else two + points
-            for e in range(4):
-                for c in range(chunks):
-                    ext[e, c, pl.ds(lo, two)] = jnp.zeros((two, LANES), F32)
+            low = 0 if side == 0 else 2 * points
+            for c in range(chunks):
+                ext0[c, pl.ds(lo, two)] = jnp.zeros((two, LANES), F32)
+                for e in range(2):
+                    ext[e, c, pl.ds(low, points)] = jnp.zeros((points, LANES), F32)
             nbr_v[1 + side] = jnp.zeros((nb, points), jnp.int32)
             cls_v[1 + side] = jnp.zeros((1, points), jnp.int32)
-            pnt_h[side] = jnp.zeros((1, points), F32)
-            sang_h[side] = jnp.zeros((1, points), F32)
-            chalo[side] = jnp.zeros((HALO, LANES), F32)
+            pnt_h[side] = jnp.zeros((2, 1, points), F32)
+            sang_h[side] = jnp.zeros((2, 1, points), F32)
+            chalo[side] = jnp.zeros((two, LANES), F32)
 
     for cp in small:
         cp.wait()
@@ -121,37 +127,56 @@
             src_ref=src, dst_ref=dst, send_sem=ssem, recv_sem=rsem, device_id=dev, device_id_type=MESH
         )
 
+    NEAR = (pl.ds(HALO, HALO), pl.ds(0, HALO))
+    FAR = (pl.ds(0, HALO), pl.ds(HALO, HALO))
+    OWN_NEAR = (pl.ds(0, HALO), pl.ds(points - HALO, HALO))
+    OWN_FAR = (pl.ds(HALO, HALO), pl.ds(points - two, HALO))
+    PAIR = pl.ds(1, 2)
+
     def meta(side):
         dev = sides[side][1]
         far = 1 - side
-        rows = pl.ds(0, HALO) if side == 0 else pl.ds(points - HALO, HALO)
+        pairs = (
+            (nbr_v.at[0], nbr_v.at[1 + far]),
+            (cown.at[OWN_NEAR[side]], chalo.at[far, NEAR[far]]),
+            (cls_v.at[0], cls_v.at[1 + far]),
+            (cown.at[OWN_FAR[side]], chalo.at[far, FAR[far]]),
+            (pnt_v.at[PAIR], pnt_h.at[far]),
+            (sang_v.at[PAIR], sang_h.at[far]),
+        )
         return [
-            remote(nbr_v.at[0], nbr_v.at[1 + far], meta_send.at[side, 0], meta_recv.at[far, 0], dev),
-            remote(cown.at[rows], chalo.at[far], meta_send.at[side, 1], meta_recv.at[far, 1], dev),
-            remote(cls_v.at[0], cls_v.at[1 + far], meta_send.at[side, 2], meta_recv.at[far, 2], dev),
-            remote(pnt_v.at[2], pnt_h.at[far], meta_send.at[side, 3], meta_recv.at[far, 3], dev),
-            remote(sang_v.at[2], sang_h.at[far], meta_send.at[side, 4], meta_recv.at[far, 4], dev),
+            remote(src, dst, meta_send.at[side, k], meta_recv.at[far, k], dev)
+            for k, (src, dst) in enumerate(pairs)
         ]
+
+    def slot(e, c, rows):
+        return ext0.at[c, rows] if e == 0 else ext.at[e - 1, c, rows]
 
     def halo(e, c, side):
         dev = sides[side][1]
         far = 1 - side
-        src = pl.ds(two, two) if side == 0 else pl.ds(points, two)
-        dst = pl.ds(two + points, two) if side == 0 else pl.ds(0, two)
-        return remote(
-            ext.at[e, c, src], ext.at[e, c, dst], send_sem.at[e, side, c], recv_sem.at[e, far, c], dev
-        )
+        if e == 0:
+            src = pl.ds(two, two) if side == 0 else pl.ds(points, two)
+            dst = pl.ds(two + points, two) if side == 0 else pl.ds(0, two)
+        else:
+            src = pl.ds(points, points)
+            dst = pl.ds(2 * points, points) if side == 0 else pl.ds(0, points)
+        return remote(slot(e, c, src), slot(e, c, dst), send_sem.at[e, side, c], recv_sem.at[e, far, c], dev)
 
     def arrival(e, c, side):
         dev = sides[side][1]
-        dst = pl.ds(0, two) if side == 0 else pl.ds(two + points, two)
-        return remote(
-            ext.at[e, c, dst], ext.at[e, c, dst], send_sem.at[e, side, c], recv_sem.at[e, side, c], dev
-        )
+        if e == 0:
+            dst = pl.ds(0, two) if side == 0 else pl.ds(two + points, two)
+        else:
+            dst = pl.ds(0, points) if side == 0 else pl.ds(2 * points, points)
+        return remote(slot(e, c, dst), slot(e, c, dst), send_sem.at[e, side, c], recv_sem.at[e, side, c], dev)
 
     def meta_arrival(side, k):
         dev = sides[side][1]
-        ref = (nbr_v.at[1 + side], chalo.at[side], cls_v.at[1 + side], pnt_h.at[side], sang_h.at[side])[k]
+        ref = (
+            nbr_v.at[1 + side], chalo.at[side, NEAR[side]], cls_v.at[1 + side],
+            chalo.at[side, FAR[side]], pnt_h.at[side], sang_h.at[side],
+        )[k]
         return remote(ref, ref, meta_send.at[side, k], meta_recv.at[side, k], dev)
 
     def sections(o):
@@ -169,12 +194,30 @@
     for o in range(1, n_sec):
         for cp in sections(o):
             cp.start()
+    held = (
+        jnp.logical_and(lax.rem(t, ROW) == 0, lax.rem(t, PLANE) != 0),
+        jnp.logical_and(lax.rem(t, ROW) == ROW - 1, lax.rem(t, PLANE) != PLANE - 1),
+    )
     for c in range(chunks):
         loads[c].wait()
         for side, (there, _) in enumerate(sides):
-            @pl.when(there)
+            @pl.when(jnp.logical_and(there, jnp.logical_not(held[side])))
             def _():
                 halo(0, c, side).start()
+    for side, (there, _) in enumerate(sides):
+        @pl.when(jnp.logical_and(there, jnp.logical_not(held[side])))
+        def _():
+            meta(side)[3].start()
+
+    for o in range(1, n_sec):
+        for cp in sections(o):
+            cp.wait_recv()
+    for side, (there, _) in enumerate(sides):
+        @pl.when(jnp.logical_and(there, held[side]))
+        def _():
+            for c in range(chunks):
+                halo(0, c, side).start()
+            meta(side)[3].start()
 
     for side, (there, _) in enumerate(sides):
         @pl.when(there)
@@ -184,34 +227,39 @@
     for k in range(3):
         tbuf[pl.ds(k * nb, nb), pl.ds(0, points)] = nbr_v[k].astype(F32)
     cols = jnp.transpose(tbuf[...])
+    half = wide // 2
     col_id = lax.broadcasted_iota(jnp.int32, (mid, 2 * LANES), 1).astype(F32)
     for n in range(nb):
         own = cols[0:points, n : n + 1]
-        left = cols[points - HALO : points, nb + n : nb + n + 1]
-        right = cols[0:HALO, 2 * nb + n : 2 * nb + n + 1]
-        at1 = jnp.concatenate([left - two, own + HALO, right + (points + HALO)], axis=0)
+        left = cols[points - two : points, nb + n : nb + n + 1]
+        right = cols[0:two, 2 * nb + n : 2 * nb + n + 1]
+        at1 = jnp.concatenate([left[HALO:] - two, own + HALO, right[:HALO] + (points + HALO)], axis=0)
         oh1[pl.ds(n * mid, mid)] = (col_id == at1).astype(F32).astype(BF16)
         oh2[pl.ds(n * points, points)] = (col_id[0:points] == own).astype(F32).astype(BF16)
-    narrow = jnp.concatenate([chalo[0], cown[...], chalo[1]], axis=0)
-    lane = lax.broadcasted_iota(jnp.int32, (mid, LANES), 1)
-    total = jnp.zeros((mid, LANES), F32)
-    for n in range(nb):
-        only = jnp.where(lane // nd == n, narrow, 0.0)
-        step = nd
-        while step < LANES:
-            only = only + pltpu.roll(only, step, 1)
-            step *= 2
-        cf[n] = only
-        total = total + only
-    csum[...] = total
-
-    for o in range(1, n_sec):
-        for cp in sections(o):
-            cp.wait_recv()
+        at3 = jnp.concatenate([left - HALO, own + two, right + (points + two)], axis=0)
+        oh3[0, pl.ds(n * half, half)] = (col_id[0:half] == at3[0:half]).astype(F32).astype(BF16)
+        oh3[1, pl.ds(n * half, half)] = (col_id[0:half] == at3[half:] - half).astype(F32).astype(BF16)
+
+    def spread_coefs(lo, narrow):
+        rows = narrow.shape[0]
+        lane = lax.broadcasted_iota(jnp.int32, (rows, LANES), 1)
+        both = jnp.zeros((rows, LANES), F32)
+        for n in range(nb):
+            only = jnp.where(lane // nd == n, narrow, 0.0)
+            step = nd
+            while step < LANES:
+                only = only + pltpu.roll(only, step, 1)
+                step *= 2
+            cf[n, pl.ds(lo, rows)] = only
+            both = both + only
+        csum[pl.ds(lo, rows)] = both
+
+    spread_coefs(HALO, jnp.concatenate([chalo[0, NEAR[0]], cown[...], chalo[1, NEAR[1]]], axis=0))
+
     for side, (there, _) in enumerate(sides):
         @pl.when(there)
         def _():
-            for cp in meta(side)[3:]:
+            for cp in meta(side)[4:]:
                 cp.start()
     for k in range(n_sec):
         tbuf[pl.ds(k, 1), pl.ds(0, points)] = pnt_v[k]
@@ -228,8 +276,8 @@
         return ttr[rows[0] : rows[1], k : k + 1]
 
     dir3[0] = column(0) * (sin_p * column(8) - cos_p * column(16))
-    dir3[1] = column(1) * jnp.maximum(cos_t * column(9) + sin_t * column(17), 0.0)
-    dir3[2] = column(3) * (1.0 + 0.5 * (cos_t * column(11) + sin_t * column(19)))
+    dir1[pl.ds(HALO, points)] = column(1) * jnp.maximum(cos_t * column(9) + sin_t * column(17), 0.0)
+    dir3[1] = column(3) * (1.0 + 0.5 * (cos_t * column(11) + sin_t * column(19)))
     dir2[pl.ds(two, points)] = column(2) * (1.0 + 0.5 * (cos_t * column(10) + sin_t * column(18)))
 
     expand = (
@@ -266,19 +314,31 @@
         near = res[:, :LANES] + res[:, LANES:]
         return [near[n * rows : (n + 1) * rows] for n in range(nb)]
 
-    def advect_twice(field, c):
+    def advected(onehot, field, mine, c, lo):
+        rows = mine.shape[0]
+        at = pl.ds(lo, rows)
         speed = con[pl.ds(8 + c, 1), :]
-        near = gathered(oh1[...], field, mid)
-        flux = near[0] * cf[0]
+        near = gathered(onehot, field, rows)
+        flux = near[0] * cf[0, at]
         for n in range(1, nb):
-            flux = flux + near[n] * cf[n]
-        first = field[HALO : HALO + mid] * (1.0 - speed * csum[...]) + speed * flux
-        near = gathered(oh2[...], first, points)
-        inner = pl.ds(HALO, points)
-        flux = near[0] * cf[0, inner]
-        for n in range(1, nb):
-            flux = flux + near[n] * cf[n, inner]
-        return first[HALO : HALO + points] * (1.0 - speed * csum[inner]) + speed * flux
+            flux = flux + near[n] * cf[n, at]
+        return mine + speed * (flux - csum[at] * mine)
+
+    def advect_far(field, c):
+        reach = half + two
+        return jnp.concatenate(
+            [
+                advected(oh3[0], field[0:reach], field[HALO : HALO + half], c, 0),
+                advected(oh3[1], field[half : half + reach], field[HALO + half : HALO + wide], c, half),
+            ],
+            axis=0,
+        )
+
+    def advect_wide(field, c):
+        return advected(oh1[...], field, field[HALO : HALO + mid], c, HALO)
+
+    def advect_own(field, c):
+        return advected(oh2[...], field, field[HALO : HALO + points], c, two)
 
     lane_own = lax.broadcasted_iota(jnp.int32, (points, LANES), 1) % nd
 
@@ -289,15 +349,15 @@
                 arrival(e, c, side).wait_recv()
 
     def hand_on(e, c, value):
-        ext[e + 1, c, own_rows] = value
+        ext[e - 1, c, pl.ds(points, points)] = value
         for side, (there, _) in enumerate(sides):
             @pl.when(there)
             def _():
-                halo(e + 1, c, side).start()
-
-    def section0(c, carry):
+                halo(e, c, side).start()
+
+    def first_leg(c, carry):
         wait_halo(0, c)
-        field = advect_twice(ext[0, c], c)
+        field = advect_own(advect_wide(ext0[c], c), c)
         turning = strength(0, c, own_rows) * dir3[0]
         following = jnp.where(
             lane_own == nd - 1, pltpu.roll(field, nd - 1, 1), pltpu.roll(field, LANES - 1, 1)
@@ -306,66 +366,76 @@
         before = jnp.where(
             lane_own == 0, pltpu.roll(faces, LANES - nd + 1, 1), pltpu.roll(faces, 1, 1)
         )
-        hand_on(0, c, field - (faces - before))
+        hand_on(1, c, field - (faces - before))
         return carry
 
-    def section1(c, carry):
+    def second_leg(c, carry):
         wait_halo(1, c)
-        field = advect_twice(ext[1, c], c)
-        hand_on(1, c, field * jnp.exp(strength(1, c, own_rows) * dir3[1]))
+        field = advect_wide(advect_far(ext[0, c], c), c)
+        field = field * jnp.exp(strength(1, c, pl.ds(HALO, mid)) * dir1[...])
+        hand_on(2, c, advect_own(field, c))
         return carry
 
-    def section2(c, carry):
+    def third_leg(c, carry):
         ratio = con[pl.ds(8 + chunks + c, 1), :]
         h2[c] = strength(2, c, pl.ds(0, wide)) * dir2[...] * ratio
-        x3[c] = jnp.exp(-(strength(3, c, own_rows) * dir3[2]))
+        x3[c] = jnp.exp(-(strength(3, c, own_rows) * dir3[1]))
         wait_halo(2, c)
-        hand_on(2, c, advect_twice(ext[2, c], c))
+        field = advect_far(ext[1, c], c)
+        fields6[c] = field
+        total[...] = total[...] + field
         return carry
 
-    lax.fori_loop(0, chunks, section0, 0)
-    lax.fori_loop(0, chunks, section1, 0)
+    lax.fori_loop(0, chunks, first_leg, 0)
 
     for side, (there, _) in enumerate(sides):
         @pl.when(there)
         def _():
-            for k in (3, 4):
+            for k in (3, 4, 5):
                 meta_arrival(side, k).wait_recv()
+    spread_coefs(0, chalo[0, FAR[0]])
+    spread_coefs(HALO + mid, chalo[1, FAR[1]])
     for side in range(2):
-        tbuf[pl.ds(side, 1), pl.ds(0, points)] = pnt_h[side]
-        tbuf[pl.ds(8 + side, 1), pl.ds(0, points)] = jnp.cos(sang_h[side])
-        tbuf[pl.ds(16 + side, 1), pl.ds(0, points)] = jnp.sin(sang_h[side])
+        for k in range(2):
+            row = 2 * side + k
+            tbuf[pl.ds(row, 1), pl.ds(0, points)] = pnt_h[side, k]
+            tbuf[pl.ds(8 + row, 1), pl.ds(0, points)] = jnp.cos(sang_h[side, k])
+            tbuf[pl.ds(16 + row, 1), pl.ds(0, points)] = jnp.sin(sang_h[side, k])
     ttr[...] = jnp.transpose(tbuf[...])
     for side in range(2):
+        rows = (points - HALO, points) if side == 0 else (0, HALO)
+        row = 2 * side
+        along = cos_t * column(8 + row, rows) + sin_t * column(16 + row, rows)
+        dir1[pl.ds(0 if side == 0 else HALO + points, HALO)] = column(row, rows) * jnp.maximum(along, 0.0)
         rows = (points - two, points) if side == 0 else (0, two)
-        lo = 0 if side == 0 else two + points
-        dir2[pl.ds(lo, two)] = column(side, rows) * (
-            1.0 + 0.5 * (cos_t * column(8 + side, rows) + sin_t * column(16 + side, rows))
-        )
-
-    lax.fori_loop(0, chunks, section2, 0)
-
-    def add_up(c, acc):
-        wait_halo(3, c)
-        return acc + ext[3, c]
-
-    acc = lax.fori_loop(0, chunks, add_up, jnp.zeros((wide, LANES), F32))
-    level = jnp.sum(acc, axis=1, keepdims=True) * (1.0 / (nf * nd))
-    csum_w = jnp.broadcast_to(level / (1.0 + level), (wide, LANES))
-    dir2[...] = csum_w
+        row = 2 * side + 1
+        along = cos_t * column(8 + row, rows) + sin_t * column(16 + row, rows)
+        dir2[pl.ds(0 if side == 0 else two + points, two)] = column(row, rows) * (1.0 + 0.5 * along)
+    total[...] = jnp.zeros((wide, LANES), F32)
+
+    lax.fori_loop(0, chunks, second_leg, 0)
+    lax.fori_loop(0, chunks, third_leg, 0)
+
+    level = jnp.sum(total[...], axis=1, keepdims=True) * (1.0 / (nf * nd))
+    total[...] = jnp.broadcast_to(level / (1.0 + level), (wide, LANES))
 
     def result(c):
         return pltpu.make_async_copy(
             outv.at[c], out.at[0, :, pl.ds(pl.multiple_of(c * LANES, LANES), LANES)], out_sem.at[c]
         )
 
-    def section3(c, carry):
-        field = ext[3, c] / (1.0 + h2[c] * dir2[...])
-        outv[c] = advect_twice(field, c) * x3[c]
-        result(c).start()
+    def last_leg(group, carry):
+        for k in range(GROUP):
+            c = group * GROUP + k
+            fields7[c] = advect_wide(fields6[c] / (1.0 + h2[c] * total[...]), c)
+        for k in range(GROUP):
+            c = group * GROUP + k
+            outv[c] = advect_own(fields7[c], c) * x3[c]
+        for k in range(GROUP):
+            result(group * GROUP + k).start()
         return carry
 
-    lax.fori_loop(0, chunks, section3, 0)
+    lax.fori_loop(0, chunks // GROUP, last_leg, 0)
 
     for side, (there, _) in enumerate(sides):
         @pl.when(there)
@@ -374,7 +444,7 @@
                 cp.wait_send()
 
             def drain(c, carry):
-                for e in range(4):
+                for e in range(3):
                     halo(e, c, side).wait_send()
                 return carry
 
@@ -399,6 +469,7 @@
     rows, base = constant_rows(nf, nd, chunks)
     geo = (n_pts, n_sec, points, nd, nb, nc, nf, chunks, base)
     two = 2 * HALO
+    full = points + 6 * HALO
     wide = points + 2 * two
     mid = points + 2 * HALO
     hbm = pl.BlockSpec(memory_space=pltpu.HBM)
@@ -412,8 +483,12 @@
         in_specs=[hbm] * 10,
         out_specs=hbm,
         scratch_shapes=[
-            vmem((4, chunks, wide, LANES), F32),
+            vmem((chunks, wide, LANES), F32),
+            vmem((2, chunks, full, LANES), F32),
             vmem((chunks, points, LANES), F32),
+            vmem((chunks, wide, LANES), F32),
+            vmem((chunks, mid, LANES), F32),
+            vmem((wide, LANES), F32),
             vmem((3, nb, points), i32),
             vmem((nb, nd, points), i32),
             vmem((nb, points), F32),
@@ -422,29 +497,31 @@
             vmem((n_sec, nc, nf), F32),
             vmem((n_sec, 1, points), F32),
             vmem((n_sec, 1, points), F32),
-            vmem((2, 1, points), F32),
-            vmem((2, 1, points), F32),
+            vmem((2, 2, 1, points), F32),
+            vmem((2, 2, 1, points), F32),
             vmem(rows.shape, F32),
             vmem((points, LANES), F32),
-            vmem((2, HALO, LANES), F32),
+            vmem((2, two, LANES), F32),
             vmem((LANES, LANES), F32),
             vmem((LANES, LANES), F32),
-            vmem((nb, mid, LANES), F32),
-            vmem((mid, LANES), F32),
+            vmem((nb, wide, LANES), F32),
+            vmem((wide, LANES), F32),
             vmem((nb * mid, 2 * LANES), BF16),
             vmem((nb * points, 2 * LANES), BF16),
+            vmem((2, nb * (wide // 2), 2 * LANES), BF16),
             vmem((wide, 3 * nc), BF16),
             vmem((n_sec, chunks, 3 * nc, LANES), BF16),
-            vmem((3, points, LANES), F32),
+            vmem((2, points, LANES), F32),
+            vmem((mid, LANES), F32),
             vmem((wide, LANES), F32),
             vmem((chunks, wide, LANES), F32),
             vmem((chunks, points, LANES), F32),
             dma((chunks,)),
             dma((9,)),
-            dma((4, 2, chunks)),
-            dma((4, 2, chunks)),
-            dma((2, 5)),
-            dma((2, 5)),
+            dma((3, 2, chunks)),
+            dma((3, 2, chunks)),
+            dma((2, 6)),
+            dma((2, 6)),
             dma((n_sec - 1, 3)),
             dma((n_sec - 1, 3)),
             dma((chunks,)),

time: 56.2 us -> 50.6 us (0.900)
  the two profiles are of different devices: /device:TPU:6 before, /device:TPU:324 now
where the time goes in v2:
time: 50.6 us; the launch traced here: 50.4 us
  Pallas kernels  48.6 us (96%)
  local copies, waits for them, and re-layouts  1.8 us (4%)
    pallas_call x1, Pallas kernels, local(): pl.pallas_call(functools.partial(kernel, geo), name='wave_window', out_sh...  48.6 us
    unnamed x1, local copies, waits for them, and re-layouts  1.8 us

profile of v2, /device:TPU:324, one launch (start us, length us, event | category | flops | bytes accessed | tf_op | source)
XLA Modules:
  0.0 50.4 jit_solution(15055965378732005287)
XLA Ops:
  0.0 48.6 %wave_window.1 = f32[1,96,1152]{2,1,0:T(8,128)} custom-call(f32[1,96,1152]{2,1,0:T(8,128)} %spec.1, s32[4,96]{1,0:T(4,128)} %nbr.1, s32[4,32,96]{2,1,0:T(8,128)} %upw.1, f32[4,96]{1,0:T(4,128)} %wgt.1, f32[4,96]{1,0:T(4,128)} %ang.1, s32[1,96]{1,0:T(1,128)} %bitcast.1, f32[1,8,36]{2,1,0:T(8,128)} %tab.1, f32[1,96]{1,0:T(1,128)} %pnt.1, f32[1,96]{1,0:T(1,128)} %sang.1, ...), custom_call_target="tpu_custom_call" | custom-call | tf_op jit(solution)/shard_map/wave_window/pallas_call | solution.py:479
  48.6 1.8 %copy.12 = f32[1,96,1152]{2,1,0:T(8,128)} copy(f32[1,96,1152]{2,1,0:T(8,128)} %wave_window.1) | data formatting | bytes 884736

commit v3 on v2

--- a/solution.py
+++ b/solution.py
@@ -13,7 +13,6 @@
 LANES = 128
 GROUP = 9
 ROW = 8
-PLANE = 32
 MESH = pl.DeviceIdType.MESH
 F32 = jnp.float32
 BF16 = jnp.bfloat16
@@ -46,9 +45,11 @@
 
 def kernel(
     geo, spec, nbr, upw, wgt, ang, cls, tab, pnt, sang, consts, out,
-    ext0, ext, outv, fields6, fields7, total, nbr_v, upw_v, wgt_v, ang_v, cls_v, tab_v, pnt_v, sang_v, pnt_h, sang_h, con,
+    ext0, ext, outv, fields6, fields7, total, nbr_v, upw_v, wgt_v, ang_v, cls_v, tab_v, pnt_v, sang_v, pnt_x, sang_x,
+    pnt_h, sang_h, con,
     cown, chalo, tbuf, ttr, cf, csum, oh1, oh2, oh3, ohc, tw, dir3, dir1, dir2, h2, x3,
-    load_sem, small_sem, send_sem, recv_sem, meta_send, meta_recv, sec_send, sec_recv, out_sem,
+    load_sem, small_sem, send_sem, recv_sem, meta_send, meta_recv, pair_send, pair_recv, sec_send, sec_recv,
+    help_send, help_recv, out_sem,
 ):
     n_pts, n_sec, points, nd, nb, nc, nf, chunks, base = geo
     two = 2 * HALO
@@ -60,16 +61,30 @@
     has_l = t > 0
     has_r = t < n_pts - 1
     sides = ((has_l, {"pts": t - 1}), (has_r, {"pts": t + 1}))
+    place = lax.rem(t, ROW)
+    served = (place == 0, place == ROW - 1)
+    helping = (place == 1, place == ROW - 2)
+    is_served = jnp.logical_or(served[0], served[1])
+    is_helping = jnp.logical_or(helping[0], helping[1])
+    direct = jnp.logical_not(is_served)
+    beside = {"section": s + 1 - 2 * lax.rem(s, 2)}
+    far_pair = 2 * (1 - lax.div(s, 2))
+    late = s < 2
+    early = jnp.logical_not(late)
 
     barrier = pltpu.get_barrier_semaphore()
     for there, dev in sides:
         @pl.when(there)
         def _():
             pl.semaphore_signal(barrier, inc=1, device_id=dev, device_id_type=MESH)
-    for o in range(1, n_sec):
-        pl.semaphore_signal(
-            barrier, inc=1, device_id={"section": lax.rem(s + o, n_sec)}, device_id_type=MESH
-        )
+    pl.semaphore_signal(barrier, inc=1, device_id=beside, device_id_type=MESH)
+
+    @pl.when(direct)
+    def _():
+        for k in range(2):
+            pl.semaphore_signal(
+                barrier, inc=1, device_id={"section": far_pair + k}, device_id_type=MESH
+            )
 
     small = [
         pltpu.make_async_copy(upw, upw_v, small_sem.at[0]),
@@ -120,7 +135,8 @@
         tbuf[pl.ds(n * nd, nd), pl.ds(0, points)] = upw_v[n].astype(F32) * wgt_v[n : n + 1, :] * along
     cown[...] = jnp.transpose(tbuf[...])[0:points]
 
-    pl.semaphore_wait(barrier, n_sec - 1 + has_l.astype(jnp.int32) + has_r.astype(jnp.int32))
+    peers = 1 + 2 * direct.astype(jnp.int32)
+    pl.semaphore_wait(barrier, peers + has_l.astype(jnp.int32) + has_r.astype(jnp.int32))
 
     def remote(src, dst, ssem, rsem, dev):
         return pltpu.make_async_remote_copy(
@@ -131,7 +147,6 @@
     FAR = (pl.ds(0, HALO), pl.ds(HALO, HALO))
     OWN_NEAR = (pl.ds(0, HALO), pl.ds(points - HALO, HALO))
     OWN_FAR = (pl.ds(HALO, HALO), pl.ds(points - two, HALO))
-    PAIR = pl.ds(1, 2)
 
     def meta(side):
         dev = sides[side][1]
@@ -141,8 +156,10 @@
             (cown.at[OWN_NEAR[side]], chalo.at[far, NEAR[far]]),
             (cls_v.at[0], cls_v.at[1 + far]),
             (cown.at[OWN_FAR[side]], chalo.at[far, FAR[far]]),
-            (pnt_v.at[PAIR], pnt_h.at[far]),
-            (sang_v.at[PAIR], sang_h.at[far]),
+            (pnt_v.at[1], pnt_h.at[far, 0]),
+            (sang_v.at[1], sang_h.at[far, 0]),
+            (pnt_v.at[2], pnt_h.at[far, 1]),
+            (sang_v.at[2], sang_h.at[far, 1]),
         )
         return [
             remote(src, dst, meta_send.at[side, k], meta_recv.at[far, k], dev)
@@ -175,49 +192,122 @@
         dev = sides[side][1]
         ref = (
             nbr_v.at[1 + side], chalo.at[side, NEAR[side]], cls_v.at[1 + side],
-            chalo.at[side, FAR[side]], pnt_h.at[side], sang_h.at[side],
+            chalo.at[side, FAR[side]], pnt_h.at[side, 0], sang_h.at[side, 0], pnt_h.at[side, 1], sang_h.at[side, 1],
         )[k]
         return remote(ref, ref, meta_send.at[side, k], meta_recv.at[side, k], dev)
 
-    def sections(o):
-        dev = {"section": lax.rem(s + o, n_sec)}
-        return [
-            remote(ref.at[s], ref.at[s], sec_send.at[o - 1, k], sec_recv.at[o - 1, k], dev)
+    def beside_copies():
+        return [
+            remote(ref.at[s], ref.at[s], pair_send.at[k], pair_recv.at[k], beside)
             for k, ref in enumerate((tab_v, pnt_v, sang_v))
         ]
+
+    def sections(k):
+        mine = lax.rem(s, 2)
+        return [
+            remote(ref.at[s], ref.at[s], sec_send.at[k, j], sec_recv.at[mine, j], {"section": far_pair + k})
+            for j, ref in enumerate((tab_v, pnt_v, sang_v))
+        ]
+
+    def section_arrivals(k):
+        return [
+            remote(ref.at[far_pair + k], ref.at[far_pair + k], sec_send.at[k, j], sec_recv.at[k, j],
+                   {"section": far_pair + k})
+            for j, ref in enumerate((tab_v, pnt_v, sang_v))
+        ]
+
+    def passed_on(k):
+        mine = lax.rem(s, 2)
+        return [
+            remote(ref.at[s], ref.at[s], sec_send.at[k, 3 + j], sec_recv.at[mine, 3 + j],
+                   {"section": far_pair + k})
+            for j, ref in enumerate((pnt_x, sang_x))
+        ]
+
+    def passed_arrivals(k):
+        return [
+            remote(ref.at[far_pair + k], ref.at[far_pair + k], sec_send.at[k, 3 + j], sec_recv.at[k, 3 + j],
+                   {"section": far_pair + k})
+            for j, ref in enumerate((pnt_x, sang_x))
+        ]
+
+    def asked(side):
+        dev = sides[side][1]
+        return [
+            remote(src.at[s], dst.at[s], help_send.at[k], help_recv.at[k], dev)
+            for k, (src, dst) in enumerate(((pnt_v, pnt_x), (sang_v, sang_x)))
+        ]
+
+    def answered(side):
+        dev = sides[side][1]
+        pair = pl.ds(far_pair, 2)
+        return [
+            remote(src.at[pair], dst.at[pair], help_send.at[2 + k], help_recv.at[2 + k], dev)
+            for k, (src, dst) in enumerate(((pnt_x, pnt_v), (sang_x, sang_v), (tab_v, tab_v)))
+        ]
+
+    def answer():
+        @pl.when(is_helping)
+        def _():
+            for k in range(2):
+                for cp in section_arrivals(k) + passed_arrivals(k):
+                    cp.wait_recv()
+
+        for side in range(2):
+            @pl.when(helping[side])
+            def _():
+                for cp in answered(side):
+                    cp.start()
+
+    def far_data():
+        @pl.when(jnp.logical_and(direct, jnp.logical_not(is_helping)))
+        def _():
+            for k in range(2):
+                for cp in section_arrivals(k):
+                    cp.wait_recv()
+
+        @pl.when(is_served)
+        def _():
+            for cp in answered(0):
+                cp.wait_recv()
+
+    for cp in beside_copies():
+        cp.start()
+    for side in range(2):
+        @pl.when(served[1 - side])
+        def _():
+            for cp in asked(side):
+                cp.start()
 
     for side, (there, _) in enumerate(sides):
         @pl.when(there)
         def _():
             for cp in meta(side)[:3]:
                 cp.start()
-    for o in range(1, n_sec):
-        for cp in sections(o):
-            cp.start()
-    held = (
-        jnp.logical_and(lax.rem(t, ROW) == 0, lax.rem(t, PLANE) != 0),
-        jnp.logical_and(lax.rem(t, ROW) == ROW - 1, lax.rem(t, PLANE) != PLANE - 1),
-    )
+    @pl.when(direct)
+    def _():
+        for k in range(2):
+            for cp in sections(k):
+                cp.start()
+
     for c in range(chunks):
         loads[c].wait()
         for side, (there, _) in enumerate(sides):
-            @pl.when(jnp.logical_and(there, jnp.logical_not(held[side])))
+            @pl.when(there)
             def _():
                 halo(0, c, side).start()
     for side, (there, _) in enumerate(sides):
-        @pl.when(jnp.logical_and(there, jnp.logical_not(held[side])))
+        @pl.when(there)
         def _():
             meta(side)[3].start()
 
-    for o in range(1, n_sec):
-        for cp in sections(o):
+    @pl.when(is_helping)
+    def _():
+        for cp in asked(0):
             cp.wait_recv()
-    for side, (there, _) in enumerate(sides):
-        @pl.when(jnp.logical_and(there, held[side]))
-        def _():
-            for c in range(chunks):
-                halo(0, c, side).start()
-            meta(side)[3].start()
+        for k in range(2):
+            for cp in passed_on(k):
+                cp.start()
 
     for side, (there, _) in enumerate(sides):
         @pl.when(there)
@@ -256,43 +346,55 @@
 
     spread_coefs(HALO, jnp.concatenate([chalo[0, NEAR[0]], cown[...], chalo[1, NEAR[1]]], axis=0))
 
-    for side, (there, _) in enumerate(sides):
-        @pl.when(there)
-        def _():
-            for cp in meta(side)[4:]:
-                cp.start()
-    for k in range(n_sec):
-        tbuf[pl.ds(k, 1), pl.ds(0, points)] = pnt_v[k]
-        phi = sang_v[k]
-        tbuf[pl.ds(8 + k, 1), pl.ds(0, points)] = jnp.cos(phi)
-        tbuf[pl.ds(16 + k, 1), pl.ds(0, points)] = jnp.sin(phi)
-    for k in range(3):
-        tbuf[pl.ds(24 + k, 1), pl.ds(0, points)] = cls_v[k].astype(F32)
-    ttr[...] = jnp.transpose(tbuf[...])
+    for cp in beside_copies():
+        cp.wait_recv()
+    pl.when(early)(answer)
+    pl.when(early)(far_data)
+
+    def relay(which):
+        for side, (there, _) in enumerate(sides):
+            @pl.when(there)
+            def _():
+                for k in (4, 5) if which == 0 else (6, 7):
+                    meta(side)[k].start()
+
+    relay(0)
     cos_t, sin_t = con[0:1], con[1:2]
     cos_p, sin_p = con[2:3], con[3:4]
 
     def column(k, rows=(0, points)):
         return ttr[rows[0] : rows[1], k : k + 1]
 
-    dir3[0] = column(0) * (sin_p * column(8) - cos_p * column(16))
-    dir1[pl.ds(HALO, points)] = column(1) * jnp.maximum(cos_t * column(9) + sin_t * column(17), 0.0)
-    dir3[1] = column(3) * (1.0 + 0.5 * (cos_t * column(11) + sin_t * column(19)))
-    dir2[pl.ds(two, points)] = column(2) * (1.0 + 0.5 * (cos_t * column(10) + sin_t * column(18)))
+    def to_columns(ks):
+        for k in ks:
+            tbuf[pl.ds(k, 1), pl.ds(0, points)] = pnt_v[k]
+            phi = sang_v[k]
+            tbuf[pl.ds(8 + k, 1), pl.ds(0, points)] = jnp.cos(phi)
+            tbuf[pl.ds(16 + k, 1), pl.ds(0, points)] = jnp.sin(phi)
 
     expand = (
         lax.broadcasted_iota(jnp.int32, (nf, nf * nd), 0)
         == lax.broadcasted_iota(jnp.int32, (nf, nf * nd), 1) // nd
     ).astype(F32).astype(BF16)
-    for k in range(n_sec):
-        table = tab_v[k]
-        hi = table.astype(BF16).astype(F32)
-        md = (table - hi).astype(BF16).astype(F32)
-        lo = table - hi - md
-        parts = jnp.concatenate([hi, md, lo], axis=0).astype(BF16)
-        spread_out = jnp.dot(parts, expand, preferred_element_type=F32)
-        for c in range(chunks):
-            tw[k, c] = spread_out[:, c * LANES : (c + 1) * LANES].astype(BF16)
+
+    def widen(ks):
+        for k in ks:
+            table = tab_v[k]
+            hi = table.astype(BF16).astype(F32)
+            md = (table - hi).astype(BF16).astype(F32)
+            lo = table - hi - md
+            parts = jnp.concatenate([hi, md, lo], axis=0).astype(BF16)
+            spread_out = jnp.dot(parts, expand, preferred_element_type=F32)
+            for c in range(chunks):
+                tw[k, c] = spread_out[:, c * LANES : (c + 1) * LANES].astype(BF16)
+
+    to_columns((0, 1))
+    for k in range(3):
+        tbuf[pl.ds(24 + k, 1), pl.ds(0, points)] = cls_v[k].astype(F32)
+    ttr[...] = jnp.transpose(tbuf[...])
+    dir3[0] = column(0) * (sin_p * column(8) - cos_p * column(16))
+    dir1[pl.ds(HALO, points)] = column(1) * jnp.maximum(cos_t * column(9) + sin_t * column(17), 0.0)
+    widen((0, 1))
     kid = lax.broadcasted_iota(jnp.int32, (wide, 3 * nc), 1) % nc
     classes = jnp.concatenate(
         [column(25, (points - two, points)), column(24), column(26, (0, two))], axis=0
@@ -386,34 +488,47 @@
         total[...] = total[...] + field
         return carry
 
-    lax.fori_loop(0, chunks, first_leg, 0)
-
-    for side, (there, _) in enumerate(sides):
-        @pl.when(there)
-        def _():
-            for k in (3, 4, 5):
-                meta_arrival(side, k).wait_recv()
+    lax.fori_loop(0, chunks // 2, first_leg, 0)
+    pl.when(late)(answer)
+    lax.fori_loop(chunks // 2, chunks, first_leg, 0)
+
+    pl.when(late)(far_data)
+    relay(1)
+    to_columns((2, 3))
+    ttr[...] = jnp.transpose(tbuf[...])
+    dir3[1] = column(3) * (1.0 + 0.5 * (cos_t * column(11) + sin_t * column(19)))
+    dir2[pl.ds(two, points)] = column(2) * (1.0 + 0.5 * (cos_t * column(10) + sin_t * column(18)))
+    widen((2, 3))
+
+    def neighbours(which, ks):
+        for side, (there, _) in enumerate(sides):
+            @pl.when(there)
+            def _():
+                for k in ks:
+                    meta_arrival(side, k).wait_recv()
+        for side in range(2):
+            tbuf[pl.ds(side, 1), pl.ds(0, points)] = pnt_h[side, which]
+            tbuf[pl.ds(8 + side, 1), pl.ds(0, points)] = jnp.cos(sang_h[side, which])
+            tbuf[pl.ds(16 + side, 1), pl.ds(0, points)] = jnp.sin(sang_h[side, which])
+        ttr[...] = jnp.transpose(tbuf[...])
+
+    neighbours(0, (3, 4, 5))
     spread_coefs(0, chalo[0, FAR[0]])
     spread_coefs(HALO + mid, chalo[1, FAR[1]])
     for side in range(2):
-        for k in range(2):
-            row = 2 * side + k
-            tbuf[pl.ds(row, 1), pl.ds(0, points)] = pnt_h[side, k]
-            tbuf[pl.ds(8 + row, 1), pl.ds(0, points)] = jnp.cos(sang_h[side, k])
-            tbuf[pl.ds(16 + row, 1), pl.ds(0, points)] = jnp.sin(sang_h[side, k])
-    ttr[...] = jnp.transpose(tbuf[...])
+        rows = (points - HALO, points) if side == 0 else (0, HALO)
+        along = cos_t * column(8 + side, rows) + sin_t * column(16 + side, rows)
+        dir1[pl.ds(0 if side == 0 else HALO + points, HALO)] = column(side, rows) * jnp.maximum(along, 0.0)
+    total[...] = jnp.zeros((wide, LANES), F32)
+
+    lax.fori_loop(0, chunks, second_leg, 0)
+
+    neighbours(1, (6, 7))
     for side in range(2):
-        rows = (points - HALO, points) if side == 0 else (0, HALO)
-        row = 2 * side
-        along = cos_t * column(8 + row, rows) + sin_t * column(16 + row, rows)
-        dir1[pl.ds(0 if side == 0 else HALO + points, HALO)] = column(row, rows) * jnp.maximum(along, 0.0)
         rows = (points - two, points) if side == 0 else (0, two)
-        row = 2 * side + 1
-        along = cos_t * column(8 + row, rows) + sin_t * column(16 + row, rows)
-        dir2[pl.ds(0 if side == 0 else two + points, two)] = column(row, rows) * (1.0 + 0.5 * along)
-    total[...] = jnp.zeros((wide, LANES), F32)
-
-    lax.fori_loop(0, chunks, second_leg, 0)
+        along = cos_t * column(8 + side, rows) + sin_t * column(16 + side, rows)
+        dir2[pl.ds(0 if side == 0 else two + points, two)] = column(side, rows) * (1.0 + 0.5 * along)
+
     lax.fori_loop(0, chunks, third_leg, 0)
 
     level = jnp.sum(total[...], axis=1, keepdims=True) * (1.0 / (nf * nd))
@@ -449,8 +564,26 @@
                 return carry
 
             lax.fori_loop(0, chunks, drain, 0)
-    for o in range(1, n_sec):
-        for cp in sections(o):
+    for cp in beside_copies():
+        cp.wait_send()
+
+    @pl.when(direct)
+    def _():
+        for k in range(2):
+            for cp in sections(k):
+                cp.wait_send()
+
+    @pl.when(is_helping)
+    def _():
+        for k in range(2):
+            for cp in passed_on(k):
+                cp.wait_send()
+        for cp in answered(0):
+            cp.wait_send()
+
+    @pl.when(is_served)
+    def _():
+        for cp in asked(0):
             cp.wait_send()
 
     def finish(c, carry):
@@ -497,6 +630,8 @@
             vmem((n_sec, nc, nf), F32),
             vmem((n_sec, 1, points), F32),
             vmem((n_sec, 1, points), F32),
+            vmem((n_sec, 1, points), F32),
+            vmem((n_sec, 1, points), F32),
             vmem((2, 2, 1, points), F32),
             vmem((2, 2, 1, points), F32),
             vmem(rows.shape, F32),
@@ -520,10 +655,14 @@
             dma((9,)),
             dma((3, 2, chunks)),
             dma((3, 2, chunks)),
-            dma((2, 6)),
-            dma((2, 6)),
-            dma((n_sec - 1, 3)),
-            dma((n_sec - 1, 3)),
+            dma((2, 8)),
+            dma((2, 8)),
+            dma((3,)),
+            dma((3,)),
+            dma((2, 5)),
+            dma((2, 5)),
+            dma((5,)),
+            dma((5,)),
             dma((chunks,)),
         ],
         compiler_params=pltpu.CompilerParams(

time: 50.6 us -> 48.5 us (0.958)
  the two profiles are of different devices: /device:TPU:324 before, /device:TPU:6 now
where the time goes in v3:
time: 48.5 us; the launch traced here: 48.3 us
  Pallas kernels  46.5 us (96%)
  local copies, waits for them, and re-layouts  1.8 us (4%)
    pallas_call x1, Pallas kernels, local(): pl.pallas_call(functools.partial(kernel, geo), name='wave_window', out_sh...  46.5 us
    unnamed x1, local copies, waits for them, and re-layouts  1.8 us

profile of v3, /device:TPU:6, one launch (start us, length us, event | category | flops | bytes accessed | tf_op | source)
XLA Modules:
  0.0 48.3 jit_solution(10253845690308103706)
XLA Ops:
  0.0 46.5 %wave_window.1 = f32[1,96,1152]{2,1,0:T(8,128)} custom-call(f32[1,96,1152]{2,1,0:T(8,128)} %spec.1, s32[4,96]{1,0:T(4,128)} %nbr.1, s32[4,32,96]{2,1,0:T(8,128)} %upw.1, f32[4,96]{1,0:T(4,128)} %wgt.1, f32[4,96]{1,0:T(4,128)} %ang.1, s32[1,96]{1,0:T(1,128)} %bitcast.1, f32[1,8,36]{2,1,0:T(8,128)} %tab.1, f32[1,96]{1,0:T(1,128)} %pnt.1, f32[1,96]{1,0:T(1,128)} %sang.1, ...), custom_call_target="tpu_custom_call" | custom-call | tf_op jit(solution)/shard_map/wave_window/pallas_call | solution.py:612
  46.5 1.8 %copy.12 = f32[1,96,1152]{2,1,0:T(8,128)} copy(f32[1,96,1152]{2,1,0:T(8,128)} %wave_window.1) | data formatting | bytes 884736

commit v4 on v3

--- a/solution.py
+++ b/solution.py
@@ -309,26 +309,21 @@
             for cp in passed_on(k):
                 cp.start()
 
-    for side, (there, _) in enumerate(sides):
-        @pl.when(there)
-        def _():
-            for k in range(3):
-                meta_arrival(side, k).wait_recv()
-    for k in range(3):
-        tbuf[pl.ds(k * nb, nb), pl.ds(0, points)] = nbr_v[k].astype(F32)
+    half = wide // 2
+    col_id = lax.broadcasted_iota(jnp.int32, (points, 2 * LANES), 1).astype(F32)
+
+    def onehot(at):
+        return (col_id[0 : at.shape[0]] == at).astype(F32).astype(BF16)
+
+    for n in range(nb):
+        tbuf[pl.ds(n, 1), pl.ds(0, points)] = nbr_v[0, pl.ds(n, 1)].astype(F32)
     cols = jnp.transpose(tbuf[...])
-    half = wide // 2
-    col_id = lax.broadcasted_iota(jnp.int32, (mid, 2 * LANES), 1).astype(F32)
     for n in range(nb):
         own = cols[0:points, n : n + 1]
-        left = cols[points - two : points, nb + n : nb + n + 1]
-        right = cols[0:two, 2 * nb + n : 2 * nb + n + 1]
-        at1 = jnp.concatenate([left[HALO:] - two, own + HALO, right[:HALO] + (points + HALO)], axis=0)
-        oh1[pl.ds(n * mid, mid)] = (col_id == at1).astype(F32).astype(BF16)
-        oh2[pl.ds(n * points, points)] = (col_id[0:points] == own).astype(F32).astype(BF16)
-        at3 = jnp.concatenate([left - HALO, own + two, right + (points + two)], axis=0)
-        oh3[0, pl.ds(n * half, half)] = (col_id[0:half] == at3[0:half]).astype(F32).astype(BF16)
-        oh3[1, pl.ds(n * half, half)] = (col_id[0:half] == at3[half:] - half).astype(F32).astype(BF16)
+        oh1[pl.ds(n * mid + HALO, points)] = onehot(own + HALO)
+        oh2[pl.ds(n * points, points)] = onehot(own)
+        oh3[0, pl.ds(n * half + two, half - two)] = onehot(own[0 : half - two] + two)
+        oh3[1, pl.ds(n * half, half - two)] = onehot(own[half - two :] + (two - half))
 
     def spread_coefs(lo, narrow):
         rows = narrow.shape[0]
@@ -344,7 +339,7 @@
             both = both + only
         csum[pl.ds(lo, rows)] = both
 
-    spread_coefs(HALO, jnp.concatenate([chalo[0, NEAR[0]], cown[...], chalo[1, NEAR[1]]], axis=0))
+    spread_coefs(two, cown[...])
 
     for cp in beside_copies():
         cp.wait_recv()
@@ -389,17 +384,39 @@
                 tw[k, c] = spread_out[:, c * LANES : (c + 1) * LANES].astype(BF16)
 
     to_columns((0, 1))
-    for k in range(3):
-        tbuf[pl.ds(24 + k, 1), pl.ds(0, points)] = cls_v[k].astype(F32)
+    tbuf[pl.ds(24, 1), pl.ds(0, points)] = cls_v[0].astype(F32)
     ttr[...] = jnp.transpose(tbuf[...])
     dir3[0] = column(0) * (sin_p * column(8) - cos_p * column(16))
     dir1[pl.ds(HALO, points)] = column(1) * jnp.maximum(cos_t * column(9) + sin_t * column(17), 0.0)
     widen((0, 1))
-    kid = lax.broadcasted_iota(jnp.int32, (wide, 3 * nc), 1) % nc
-    classes = jnp.concatenate(
-        [column(25, (points - two, points)), column(24), column(26, (0, two))], axis=0
-    )
-    ohc[...] = (kid.astype(F32) == classes).astype(F32).astype(BF16)
+    kid = (lax.broadcasted_iota(jnp.int32, (points, 3 * nc), 1) % nc).astype(F32)
+
+    def classes(at):
+        return (kid[0 : at.shape[0]] == at).astype(F32).astype(BF16)
+
+    ohc[pl.ds(two, points)] = classes(column(24))
+
+    for side, (there, _) in enumerate(sides):
+        @pl.when(there)
+        def _():
+            for k in range(3):
+                meta_arrival(side, k).wait_recv()
+    for k in range(2 * nb):
+        tbuf[pl.ds(k, 1), pl.ds(0, points)] = nbr_v[1 + k // nb, pl.ds(k % nb, 1)].astype(F32)
+    for k in range(2):
+        tbuf[pl.ds(2 * nb + k, 1), pl.ds(0, points)] = cls_v[1 + k].astype(F32)
+    cols = jnp.transpose(tbuf[...])
+    for n in range(nb):
+        left = cols[points - two : points, n : n + 1]
+        right = cols[0:two, nb + n : nb + n + 1]
+        oh1[pl.ds(n * mid, HALO)] = onehot(left[HALO:] - two)
+        oh1[pl.ds(n * mid + HALO + points, HALO)] = onehot(right[:HALO] + (points + HALO))
+        oh3[0, pl.ds(n * half, two)] = onehot(left - HALO)
+        oh3[1, pl.ds(n * half + half - two, two)] = onehot(right + (points + two - half))
+    spread_coefs(HALO, chalo[0, NEAR[0]])
+    spread_coefs(two + points, chalo[1, NEAR[1]])
+    ohc[pl.ds(0, two)] = classes(cols[points - two : points, 2 * nb : 2 * nb + 1])
+    ohc[pl.ds(two + points, two)] = classes(cols[0:two, 2 * nb + 1 : 2 * nb + 2])
 
     def strength(k, c, rows):
         return jnp.dot(ohc[rows], tw[k, c], preferred_element_type=F32)
@@ -478,27 +495,26 @@
         hand_on(2, c, advect_own(field, c))
         return carry
 
-    def third_leg(c, carry):
+    def prepare(c):
         ratio = con[pl.ds(8 + chunks + c, 1), :]
         h2[c] = strength(2, c, pl.ds(0, wide)) * dir2[...] * ratio
         x3[c] = jnp.exp(-(strength(3, c, own_rows) * dir3[1]))
+
+    def third_leg(c, carry):
         wait_halo(2, c)
         field = advect_far(ext[1, c], c)
         fields6[c] = field
         total[...] = total[...] + field
         return carry
 
+    def third_leg_ahead(c, carry):
+        prepare(2 * (c - split))
+        prepare(2 * (c - split) + 1)
+        return third_leg(c, carry)
+
     lax.fori_loop(0, chunks // 2, first_leg, 0)
     pl.when(late)(answer)
     lax.fori_loop(chunks // 2, chunks, first_leg, 0)
-
-    pl.when(late)(far_data)
-    relay(1)
-    to_columns((2, 3))
-    ttr[...] = jnp.transpose(tbuf[...])
-    dir3[1] = column(3) * (1.0 + 0.5 * (cos_t * column(11) + sin_t * column(19)))
-    dir2[pl.ds(two, points)] = column(2) * (1.0 + 0.5 * (cos_t * column(10) + sin_t * column(18)))
-    widen((2, 3))
 
     def neighbours(which, ks):
         for side, (there, _) in enumerate(sides):
@@ -521,7 +537,19 @@
         dir1[pl.ds(0 if side == 0 else HALO + points, HALO)] = column(side, rows) * jnp.maximum(along, 0.0)
     total[...] = jnp.zeros((wide, LANES), F32)
 
-    lax.fori_loop(0, chunks, second_leg, 0)
+    lax.fori_loop(0, chunks // 2, second_leg, 0)
+
+    pl.when(late)(far_data)
+    relay(1)
+    to_columns((2, 3))
+    ttr[...] = jnp.transpose(tbuf[...])
+    dir3[1] = column(3) * (1.0 + 0.5 * (cos_t * column(11) + sin_t * column(19)))
+    dir2[pl.ds(two, points)] = column(2) * (1.0 + 0.5 * (cos_t * column(10) + sin_t * column(18)))
+    widen((2, 3))
+
+    lax.fori_loop(chunks // 2, chunks, second_leg, 0)
+    split = chunks - chunks // 2
+    lax.fori_loop(0, split, third_leg, 0)
 
     neighbours(1, (6, 7))
     for side in range(2):
@@ -529,7 +557,9 @@
         along = cos_t * column(8 + side, rows) + sin_t * column(16 + side, rows)
         dir2[pl.ds(0 if side == 0 else two + points, two)] = column(side, rows) * (1.0 + 0.5 * along)
 
-    lax.fori_loop(0, chunks, third_leg, 0)
+    for c in range(2 * (chunks - split), chunks):
+        prepare(c)
+    lax.fori_loop(split, chunks, third_leg_ahead, 0)
 
     level = jnp.sum(total[...], axis=1, keepdims=True) * (1.0 / (nf * nd))
     total[...] = jnp.broadcast_to(level / (1.0 + level), (wide, LANES))

time: 48.5 us -> 46.8 us (0.965)
  Pallas kernels: 46.5 us -> 44.8 us
    pallas_call x1, Pallas kernels: 46.5 us -> 44.8 us  [local(): pl.pallas_call(functools.partial(kernel, geo), name='wave_window', out_sh...]
where the time goes in v4:
time: 46.8 us; the launch traced here: 46.6 us
  Pallas kernels  44.8 us (96%)
  local copies, waits for them, and re-layouts  1.8 us (4%)
    pallas_call x1, Pallas kernels, local(): pl.pallas_call(functools.partial(kernel, geo), name='wave_window', out_sh...  44.8 us
    unnamed x1, local copies, waits for them, and re-layouts  1.8 us

profile of v4, /device:TPU:6, one launch (start us, length us, event | category | flops | bytes accessed | tf_op | source)
XLA Modules:
  0.0 46.6 jit_solution(550959460853019278)
XLA Ops:
  0.0 44.8 %wave_window.1 = f32[1,96,1152]{2,1,0:T(8,128)} custom-call(f32[1,96,1152]{2,1,0:T(8,128)} %spec.1, s32[4,96]{1,0:T(4,128)} %nbr.1, s32[4,32,96]{2,1,0:T(8,128)} %upw.1, f32[4,96]{1,0:T(4,128)} %wgt.1, f32[4,96]{1,0:T(4,128)} %ang.1, s32[1,96]{1,0:T(1,128)} %bitcast.1, f32[1,8,36]{2,1,0:T(8,128)} %tab.1, f32[1,96]{1,0:T(1,128)} %pnt.1, f32[1,96]{1,0:T(1,128)} %sang.1, ...), custom_call_target="tpu_custom_call" | custom-call | tf_op jit(solution)/shard_map/wave_window/pallas_call | solution.py:642
  44.8 1.8 %copy.12 = f32[1,96,1152]{2,1,0:T(8,128)} copy(f32[1,96,1152]{2,1,0:T(8,128)} %wave_window.1) | data formatting | bytes 884736

commit v5 on v4

--- a/solution.py
+++ b/solution.py
@@ -47,7 +47,7 @@
     geo, spec, nbr, upw, wgt, ang, cls, tab, pnt, sang, consts, out,
     ext0, ext, outv, fields6, fields7, total, nbr_v, upw_v, wgt_v, ang_v, cls_v, tab_v, pnt_v, sang_v, pnt_x, sang_x,
     pnt_h, sang_h, con,
-    cown, chalo, tbuf, ttr, cf, csum, oh1, oh2, oh3, ohc, tw, dir3, dir1, dir2, h2, x3,
+    cown, chalo, tbuf, ttr, cf, csum, ohf, ohm, ohw, ohc, tw, dir3, dir1, dir2, h2, x3,
     load_sem, small_sem, send_sem, recv_sem, meta_send, meta_recv, pair_send, pair_recv, sec_send, sec_recv,
     help_send, help_recv, out_sem,
 ):
@@ -309,21 +309,22 @@
             for cp in passed_on(k):
                 cp.start()
 
-    half = wide // 2
-    col_id = lax.broadcasted_iota(jnp.int32, (points, 2 * LANES), 1).astype(F32)
+    half = points // 2
 
     def onehot(at):
-        return (col_id[0 : at.shape[0]] == at).astype(F32).astype(BF16)
+        rows = at.shape[0]
+        reach = rows + two
+        lane = lax.broadcasted_iota(jnp.int32, (rows, 2 * LANES), 1)
+        pos = jnp.where(lane < reach, lane, jnp.where(lane < 2 * reach, lane - reach, -1))
+        return (pos.astype(F32) == at).astype(F32).astype(BF16)
 
     for n in range(nb):
         tbuf[pl.ds(n, 1), pl.ds(0, points)] = nbr_v[0, pl.ds(n, 1)].astype(F32)
     cols = jnp.transpose(tbuf[...])
     for n in range(nb):
         own = cols[0:points, n : n + 1]
-        oh1[pl.ds(n * mid + HALO, points)] = onehot(own + HALO)
-        oh2[pl.ds(n * points, points)] = onehot(own)
-        oh3[0, pl.ds(n * half + two, half - two)] = onehot(own[0 : half - two] + two)
-        oh3[1, pl.ds(n * half, half - two)] = onehot(own[half - two :] + (two - half))
+        ohm[0, pl.ds(n * half, half)] = onehot(own[0:half])
+        ohm[1, pl.ds(n * half, half)] = onehot(own[half:] - half)
 
     def spread_coefs(lo, narrow):
         rows = narrow.shape[0]
@@ -409,10 +410,10 @@
     for n in range(nb):
         left = cols[points - two : points, n : n + 1]
         right = cols[0:two, nb + n : nb + n + 1]
-        oh1[pl.ds(n * mid, HALO)] = onehot(left[HALO:] - two)
-        oh1[pl.ds(n * mid + HALO + points, HALO)] = onehot(right[:HALO] + (points + HALO))
-        oh3[0, pl.ds(n * half, two)] = onehot(left - HALO)
-        oh3[1, pl.ds(n * half + half - two, two)] = onehot(right + (points + two - half))
+        ohw[0, pl.ds(n * HALO, HALO)] = onehot(left[HALO:] - two)
+        ohw[1, pl.ds(n * HALO, HALO)] = onehot(right[:HALO])
+        ohf[0, pl.ds(n * two, two)] = onehot(left - HALO)
+        ohf[1, pl.ds(n * two, two)] = onehot(right)
     spread_coefs(HALO, chalo[0, NEAR[0]])
     spread_coefs(two + points, chalo[1, NEAR[1]])
     ohc[pl.ds(0, two)] = classes(cols[points - two : points, 2 * nb : 2 * nb + 1])
@@ -423,41 +424,36 @@
 
     own_rows = pl.ds(two, points)
 
-    def gathered(onehot, field, rows):
-        depth = field.shape[0]
+    def advected(pieces, field, base, c):
+        speed = con[pl.ds(8 + c, 1), :]
         hi, lo = split2(field)
-        rhs = jnp.concatenate([hi, lo], axis=1)
-        if depth < 2 * LANES:
-            rhs = jnp.concatenate([rhs, jnp.zeros((2 * LANES - depth, 2 * LANES), BF16)], axis=0)
-        res = jnp.dot(onehot, rhs, preferred_element_type=F32)
-        near = res[:, :LANES] + res[:, LANES:]
-        return [near[n * rows : (n + 1) * rows] for n in range(nb)]
-
-    def advected(onehot, field, mine, c, lo):
-        rows = mine.shape[0]
-        at = pl.ds(lo, rows)
-        speed = con[pl.ds(8 + c, 1), :]
-        near = gathered(onehot, field, rows)
-        flux = near[0] * cf[0, at]
-        for n in range(1, nb):
-            flux = flux + near[n] * cf[n, at]
-        return mine + speed * (flux - csum[at] * mine)
+        out = []
+        for select, first, rows in pieces:
+            window = slice(first - HALO - base, first - HALO - base + rows + two)
+            rhs = [hi[window], lo[window]]
+            spare = 2 * LANES - 2 * (rows + two)
+            if spare:
+                rhs.append(jnp.zeros((spare, LANES), BF16))
+            near = jnp.dot(select, jnp.concatenate(rhs, axis=0), preferred_element_type=F32)
+            at = pl.ds(first, rows)
+            flux = near[0:rows] * cf[0, at]
+            for n in range(1, nb):
+                flux = flux + near[n * rows : (n + 1) * rows] * cf[n, at]
+            mine = field[first - base : first - base + rows]
+            out.append(mine + speed * (flux - csum[at] * mine))
+        return jnp.concatenate(out, axis=0)
+
+    def inner():
+        return [(ohm[0], two, half), (ohm[1], two + half, half)]
 
     def advect_far(field, c):
-        reach = half + two
-        return jnp.concatenate(
-            [
-                advected(oh3[0], field[0:reach], field[HALO : HALO + half], c, 0),
-                advected(oh3[1], field[half : half + reach], field[HALO + half : HALO + wide], c, half),
-            ],
-            axis=0,
-        )
+        return advected([(ohf[0], 0, two)] + inner() + [(ohf[1], two + points, two)], field, -HALO, c)
 
     def advect_wide(field, c):
-        return advected(oh1[...], field, field[HALO : HALO + mid], c, HALO)
+        return advected([(ohw[0], HALO, HALO)] + inner() + [(ohw[1], two + points, HALO)], field, 0, c)
 
     def advect_own(field, c):
-        return advected(oh2[...], field, field[HALO : HALO + points], c, two)
+        return advected(inner(), field, HALO, c)
 
     lane_own = lax.broadcasted_iota(jnp.int32, (points, LANES), 1) % nd
 
@@ -505,6 +501,12 @@
         field = advect_far(ext[1, c], c)
         fields6[c] = field
         total[...] = total[...] + field
+        for side, (there, _) in enumerate(sides):
+            @pl.when(there)
+            def _():
+                for e in range(3):
+                    halo(e, c, side).wait_send()
+
         return carry
 
     def third_leg_ahead(c, carry):
@@ -552,6 +554,33 @@
     lax.fori_loop(0, split, third_leg, 0)
 
     neighbours(1, (6, 7))
+    for side, (there, _) in enumerate(sides):
+        @pl.when(there)
+        def _():
+            for cp in meta(side):
+                cp.wait_send()
+    for cp in beside_copies():
+        cp.wait_send()
+
+    @pl.when(direct)
+    def _():
+        for k in range(2):
+            for cp in sections(k):
+                cp.wait_send()
+
+    @pl.when(is_helping)
+    def _():
+        for k in range(2):
+            for cp in passed_on(k):
+                cp.wait_send()
+        for cp in answered(0):
+            cp.wait_send()
+
+    @pl.when(is_served)
+    def _():
+        for cp in asked(0):
+            cp.wait_send()
+
     for side in range(2):
         rows = (points - two, points) if side == 0 else (0, two)
         along = cos_t * column(8 + side, rows) + sin_t * column(16 + side, rows)
@@ -581,40 +610,6 @@
         return carry
 
     lax.fori_loop(0, chunks // GROUP, last_leg, 0)
-
-    for side, (there, _) in enumerate(sides):
-        @pl.when(there)
-        def _():
-            for cp in meta(side):
-                cp.wait_send()
-
-            def drain(c, carry):
-                for e in range(3):
-                    halo(e, c, side).wait_send()
-                return carry
-
-            lax.fori_loop(0, chunks, drain, 0)
-    for cp in beside_copies():
-        cp.wait_send()
-
-    @pl.when(direct)
-    def _():
-        for k in range(2):
-            for cp in sections(k):
-                cp.wait_send()
-
-    @pl.when(is_helping)
-    def _():
-        for k in range(2):
-            for cp in passed_on(k):
-                cp.wait_send()
-        for cp in answered(0):
-            cp.wait_send()
-
-    @pl.when(is_served)
-    def _():
-        for cp in asked(0):
-            cp.wait_send()
 
     def finish(c, carry):
         result(c).wait()
@@ -671,9 +666,9 @@
             vmem((LANES, LANES), F32),
             vmem((nb, wide, LANES), F32),
             vmem((wide, LANES), F32),
-            vmem((nb * mid, 2 * LANES), BF16),
-            vmem((nb * points, 2 * LANES), BF16),
-            vmem((2, nb * (wide // 2), 2 * LANES), BF16),
+            vmem((2, nb * two, 2 * LANES), BF16),
+            vmem((2, nb * points // 2, 2 * LANES), BF16),
+            vmem((2, nb * HALO, 2 * LANES), BF16),
             vmem((wide, 3 * nc), BF16),
             vmem((n_sec, chunks, 3 * nc, LANES), BF16),
             vmem((2, points, LANES), F32),

time: 46.8 us -> 46.5 us (level)
  no operation moved by 1% of the time
where the time goes in v5:
time: 46.5 us; the launch traced here: 46.3 us
  Pallas kernels  44.5 us (96%)
  local copies, waits for them, and re-layouts  1.8 us (4%)
    pallas_call x1, Pallas kernels, local(): pl.pallas_call(functools.partial(kernel, geo), name='wave_window', out_sh...  44.5 us
    unnamed x1, local copies, waits for them, and re-layouts  1.8 us

profile of v5, /device:TPU:6, one launch (start us, length us, event | category | flops | bytes accessed | tf_op | source)
XLA Modules:
  0.0 46.3 jit_solution(8632273198791910112)
XLA Ops:
  0.0 44.5 %wave_window.1 = f32[1,96,1152]{2,1,0:T(8,128)} custom-call(f32[1,96,1152]{2,1,0:T(8,128)} %spec.1, s32[4,96]{1,0:T(4,128)} %nbr.1, s32[4,32,96]{2,1,0:T(8,128)} %upw.1, f32[4,96]{1,0:T(4,128)} %wgt.1, f32[4,96]{1,0:T(4,128)} %ang.1, s32[1,96]{1,0:T(1,128)} %bitcast.1, f32[1,8,36]{2,1,0:T(8,128)} %tab.1, f32[1,96]{1,0:T(1,128)} %pnt.1, f32[1,96]{1,0:T(1,128)} %sang.1, ...), custom_call_target="tpu_custom_call" | custom-call | tf_op jit(solution)/shard_map/wave_window/pallas_call | solution.py:637
  44.5 1.8 %copy.12 = f32[1,96,1152]{2,1,0:T(8,128)} copy(f32[1,96,1152]{2,1,0:T(8,128)} %wave_window.1) | data formatting | bytes 884736

commit v6 on v5

--- a/solution.py
+++ b/solution.py
@@ -605,8 +605,9 @@
         for k in range(GROUP):
             c = group * GROUP + k
             outv[c] = advect_own(fields7[c], c) * x3[c]
-        for k in range(GROUP):
-            result(group * GROUP + k).start()
+            if k > 0:
+                result(c - 1).start()
+        result(group * GROUP + GROUP - 1).start()
         return carry
 
     lax.fori_loop(0, chunks // GROUP, last_leg, 0)

time: 46.5 us -> 46.4 us (level)
  no operation moved by 1% of the time
where the time goes in v6:
time: 46.4 us; the launch traced here: 46.2 us
  Pallas kernels  44.3 us (95%)
  local copies, waits for them, and re-layouts  1.8 us (4%)
    pallas_call x1, Pallas kernels, local(): pl.pallas_call(functools.partial(kernel, geo), name='wave_window', out_sh...  44.3 us
    unnamed x1, local copies, waits for them, and re-layouts  1.8 us

profile of v6, /device:TPU:6, one launch (start us, length us, event | category | flops | bytes accessed | tf_op | source)
XLA Modules:
  0.0 46.2 jit_solution(6854915844610326811)
XLA Ops:
  0.0 44.3 %wave_window.1 = f32[1,96,1152]{2,1,0:T(8,128)} custom-call(f32[1,96,1152]{2,1,0:T(8,128)} %spec.1, s32[4,96]{1,0:T(4,128)} %nbr.1, s32[4,32,96]{2,1,0:T(8,128)} %upw.1, f32[4,96]{1,0:T(4,128)} %wgt.1, f32[4,96]{1,0:T(4,128)} %ang.1, s32[1,96]{1,0:T(1,128)} %bitcast.1, f32[1,8,36]{2,1,0:T(8,128)} %tab.1, f32[1,96]{1,0:T(1,128)} %pnt.1, f32[1,96]{1,0:T(1,128)} %sang.1, ...), custom_call_target="tpu_custom_call" | custom-call | tf_op jit(solution)/shard_map/wave_window/pallas_call | solution.py:638
  44.3 1.8 %copy.12 = f32[1,96,1152]{2,1,0:T(8,128)} copy(f32[1,96,1152]{2,1,0:T(8,128)} %wave_window.1) | data formatting | bytes 884736
